TPU v7x, 256 devices: a whole 4x4x8 slice. The times are simulated.
256 devices in a mesh: dp: 4 (over y_lo, core), sp: 8 (over y_hi, x), tp: 8 (over z).
Axes of the slice: x: 4, y: 4 (y_hi: 2, y_lo: 2; y = y_hi * 2 + y_lo), z: 8, core: 2. Of those that a mesh axis runs over, the one named last changes fastest.
Arguments:
- query: bfloat16 [4, 3072, 3072], P('dp', 'sp', 'tp'), may hold values from -110 to 110
- key: bfloat16 [4, 3072, 3072], P('dp', 'sp', 'tp'), may hold values from -8 to 8
- value: bfloat16 [4, 3072, 3072], P('dp', 'sp', 'tp'), may hold values from -6 to 6
- text_key: bfloat16 [4, 256, 3072], P('dp', None, 'tp'), may hold values from -6 to 6
- text_value: bfloat16 [4, 256, 3072], P('dp', None, 'tp'), may hold values from -6 to 6
- grad_out: bfloat16 [4, 3072, 3072], P('dp', 'sp', 'tp'), may hold values from -6 to 6
- gate: bfloat16 [4, 3072], P('dp'), may hold values from 0.5 to 1.5
- out_weight: bfloat16 [3072, 3072], P('tp', 'dp'), may hold values from -0.109375 to 0.109375
- windows: int32 [8, 2], P('sp'), may hold values from 0 to 2, as said below
- tile_map: int32 [8, 1], replicated, may hold values from 0 to 2, as said below
- text_count: int32 [4], P('dp'), may hold values from 1 to 256
Outputs:
- grad_query: bfloat16 [4, 3072, 3072], P('dp', 'sp', 'tp')
- grad_key: bfloat16 [4, 3072, 3072], P('dp', 'sp', 'tp')
- grad_value: bfloat16 [4, 3072, 3072], P('dp', 'sp', 'tp')
- grad_text_key: bfloat16 [4, 256, 3072], P('dp', None, 'tp')
- grad_text_value: bfloat16 [4, 256, 3072], P('dp', None, 'tp')
- grad_weight: float32 [3072, 3072], P('tp', 'dp')
Inputs may be any that keep to these rules, and one draw needn't show every extreme that they name: `tile_map`: the positions within each row are distinct. `windows`: the time reach is 0 or 1; the first tile of every time slab has time reach 1 and spatial reach 2.
All inputs are finite; a program needn't handle non-finite values.
Results may differ from a plain program's by a relative error of at most 0.024.
Values may be sent and summed in bfloat16 or wider, within the bound.
No kernel may reach another device: no remote copies, remote signals or barrier semaphores. Data moves between devices by JAX's collectives and lax.ppermute only.
A program may use at most 64 MiB of HBM per device.

v0:
```python
import jax
import jax.numpy as jnp
from jax import lax
from jax.sharding import PartitionSpec as P

HD = 128
TILE = 384


def in_order(parts, dim):
    shape = list(parts.shape[1:])
    shape[dim] *= parts.shape[0]
    return jnp.moveaxis(parts, 0, dim).reshape(shape)


def from_everyone(shard, axis):
    copies = jnp.broadcast_to(shard, (lax.axis_size(axis), *shard.shape))
    return lax.all_to_all(copies, axis, split_axis=0, concat_axis=0, tiled=True)


def gathered_copies(shard, axis, dim):
    return in_order(from_everyone(shard, axis), dim)


def padded(cells, sides, width):
    for axis, dim in sides:
        count = lax.axis_size(axis)
        ends = count - 1
        head = lax.slice_in_dim(cells, 0, width, axis=dim)
        tail = lax.slice_in_dim(cells, cells.shape[dim] - width, cells.shape[dim], axis=dim)
        cells = jnp.concatenate(
            [
                lax.ppermute(tail, axis, [(i, (i + 1) % count) for i in range(ends)]),
                cells,
                lax.ppermute(head, axis, [((i + 1) % count, i) for i in range(ends)]),
            ],
            axis=dim,
        )
    return cells


def shifted(block, axis, distance):
    devices = range(lax.axis_size(axis))
    route = [(i - distance, i) for i in devices if i - distance in devices]
    return lax.ppermute(block, axis, route)


def cut_along(shard, dim, count):
    shape = shard.shape
    parts = shard.reshape(*shape[:dim], count, shape[dim] // count, *shape[dim + 1 :])
    return jnp.moveaxis(parts, dim, 0)


def summed_on_arrival(shard, axis, dim):
    count = lax.axis_size(axis)
    parts = lax.all_to_all(cut_along(shard, dim, count), axis, 0, 0, tiled=True)
    return jnp.sum(parts.astype(jnp.float32), axis=0)


def window_mask(own_map, side_maps, valid, spans, text_live):
    reach = jnp.abs(jnp.arange(3, dtype=jnp.int32) - 1)
    near_time = reach[None, :, None] <= spans[:, 0][:, None, None]
    near_space = (
        jnp.abs(own_map[:, None, None] - side_maps[None, :, :]) <= spans[:, 1][:, None, None]
    )
    allowed = near_time & near_space & valid[None, :, None]
    count = own_map.shape[0]
    tiles = allowed.reshape(count, 3 * count)
    video = jnp.broadcast_to(tiles[:, None, :, None], (count, TILE, 3 * count, TILE))
    video = video.reshape(count * TILE, 3 * count * TILE)
    text = jnp.broadcast_to(text_live[None, :], (count * TILE, text_live.shape[0]))
    return jnp.concatenate([video, text], axis=1)


def tile_attention(query, keys, values, grad_attn, allowed):
    factor = HD ** (-0.5)
    scores = factor * jnp.dot(query, keys.T, preferred_element_type=jnp.float32)
    scores = jnp.where(allowed, scores, -1e30)
    top = jnp.max(scores, axis=1, keepdims=True)
    weights = jnp.exp(scores - top)
    weights = weights / jnp.sum(weights, axis=1, keepdims=True)
    probs = weights.astype(jnp.bfloat16)
    attended = jnp.dot(probs, values, preferred_element_type=jnp.float32).astype(jnp.bfloat16)
    delta = jnp.sum(
        grad_attn.astype(jnp.float32) * attended.astype(jnp.float32), axis=1, keepdims=True
    )
    grad_probs = jnp.dot(grad_attn, values.T, preferred_element_type=jnp.float32)
    grad_scores = (weights * (grad_probs - delta)).astype(jnp.bfloat16)
    grad_query = factor * jnp.dot(grad_scores, keys, preferred_element_type=jnp.float32)
    grad_keys = factor * jnp.dot(grad_scores.T, query, preferred_element_type=jnp.float32)
    grad_values = jnp.dot(probs.T, grad_attn, preferred_element_type=jnp.float32)
    return (attended, grad_query, grad_keys, grad_values)


def per_device(
    query,
    key,
    value,
    text_key,
    text_value,
    grad_out,
    gate,
    out_weight,
    windows,
    tile_map,
    text_count,
):
    own_query = query[0]
    tok = own_query.shape[0]
    width = own_query.shape[1]
    full_grad = lax.all_gather(grad_out[0], "tp", axis=1, tiled=True)
    scaled = (full_grad.astype(jnp.float32) * gate[0].astype(jnp.float32)[None, :]).astype(
        jnp.bfloat16
    )
    grad_attn = lax.dot_general(
        scaled,
        gathered_copies(out_weight, "dp", 1),
        (((1,), (1,)), ((), ())),
        preferred_element_type=jnp.float32,
    )
    grad_attn = grad_attn.astype(jnp.bfloat16)
    paired = jnp.stack([key[0], value[0]], axis=0)
    extended = padded(paired, (("sp", 1),), tok)
    index = lax.axis_index("sp")
    slabs = lax.axis_size("sp")
    tiles_here = tile_map.shape[1]
    blank = jnp.zeros((1, tiles_here), jnp.int32)
    padded_map = jnp.concatenate([blank, tile_map, blank], axis=0)
    own_map = lax.dynamic_index_in_dim(tile_map, index, 0, keepdims=False)
    side_maps = lax.dynamic_slice_in_dim(padded_map, index, 3, 0)
    others = index + jnp.arange(3, dtype=jnp.int32) - 1
    valid = (others >= 0) & (others < slabs)
    text_live = jnp.arange(text_key.shape[1], dtype=jnp.int32) < text_count[0]
    allowed = window_mask(own_map, side_maps, valid, windows, text_live)
    results = [[], [], [], []]
    for head in range(width // HD):
        lower = head * HD
        upper = lower + HD
        all_k = jnp.concatenate([extended[0][:, lower:upper], text_key[0][:, lower:upper]], axis=0)
        all_v = jnp.concatenate(
            [extended[1][:, lower:upper], text_value[0][:, lower:upper]], axis=0
        )
        outcome = tile_attention(
            own_query[:, lower:upper], all_k, all_v, grad_attn[:, lower:upper], allowed
        )
        for place in range(4):
            results[place].append(outcome[place])
    attended = jnp.concatenate(results[0], axis=1)
    grad_q = jnp.concatenate(results[1], axis=1)
    grad_k = jnp.concatenate(results[2], axis=1)
    grad_v = jnp.concatenate(results[3], axis=1)
    earlier = jnp.stack([grad_k[:tok], grad_v[:tok]], axis=0)
    later = jnp.stack([grad_k[2 * tok : 3 * tok], grad_v[2 * tok : 3 * tok]], axis=0)
    from_later = shifted(earlier.astype(jnp.bfloat16), "sp", -1).astype(earlier.dtype)
    from_earlier = shifted(later.astype(jnp.bfloat16), "sp", 1).astype(later.dtype)
    own_k = grad_k[tok : 2 * tok] + from_later[0] + from_earlier[0]
    own_v = grad_v[tok : 2 * tok] + from_later[1] + from_earlier[1]
    text_k, text_v = (
        lax.psum(grad_k[3 * tok :].astype(jnp.bfloat16), "sp").astype(jnp.float32),
        lax.psum(grad_v[3 * tok :].astype(jnp.bfloat16), "sp").astype(jnp.float32),
    )
    local_weight = lax.dot_general(
        attended, scaled, (((0,), (0,)), ((), ())), preferred_element_type=jnp.float32
    )
    spread = summed_on_arrival(local_weight.astype(jnp.bfloat16), ("dp", "sp"), 1)
    weight_grad = gathered_copies(spread, "sp", 1)
    return (
        grad_q.astype(jnp.bfloat16)[None],
        own_k.astype(jnp.bfloat16)[None],
        own_v.astype(jnp.bfloat16)[None],
        text_k.astype(jnp.bfloat16)[None],
        text_v.astype(jnp.bfloat16)[None],
        weight_grad,
    )


def solution(mesh):
    placed = (
        P("dp", "sp", "tp"),
        P("dp", "sp", "tp"),
        P("dp", "sp", "tp"),
        P("dp", None, "tp"),
        P("dp", None, "tp"),
        P("dp", "sp", "tp"),
        P("dp", None),
        P("tp", "dp"),
        P("sp", None),
        P(),
        P("dp"),
    )
    return jax.shard_map(
        per_device,
        mesh=mesh,
        in_specs=placed,
        out_specs=(
            P("dp", "sp", "tp"),
            P("dp", "sp", "tp"),
            P("dp", "sp", "tp"),
            P("dp", None, "tp"),
            P("dp", None, "tp"),
            P("tp", "dp"),
        ),
        check_vma=False,
    )
```

profile of v0, /device:TPU:2, one launch (start us, length us, event | category | flops | bytes accessed | tf_op | source)
XLA Modules:
  0.0 224.4 jit_solution(2305887054889296009)
XLA Ops:
  9.2 4.2 %collective-permute-start.1 = (bf16[2,384,384]{2,1,0:T(8,128)(2,1)S(1)}, bf16[2,384,384]{2,1,0:T(8,128)(2,1)S(1)}, u32[]{:S(2)}, u32[]{:S(2)}) collective-permute-start(bf16[2,384,384]{2,1,0:T(8,128)(2,1)S(1)} %constant_dynamic-update-slice_fusion), channel_id=1, source_target_pairs={{8,0},{16,8},{24,16},{32,24},{40,32},{48,40},{56,48},{9,1},{17,9},... | collective-permute-start | bytes 1769480 | tf_op jit(solution)/shard_map/ppermute | solution.py:35
  13.3 1.9 collective-permute-start
  15.3 1.4 copy.25
  16.6 1.7 broadcast_in_dim.59
  18.3 4.6 %all-to-all-start = ((bf16[4,384,768]{1,2,0:T(8,128)(2,1)}), bf16[4,384,768]{1,2,0:T(8,128)(2,1)}, u32[]{:S(2)}, u32[]{:S(2)}) async-start(bf16[4,384,768]{1,2,0:T(8,128)(2,1)} %broadcast_in_dim.59), calls=%async_computation | async-start | bytes 4718592 | tf_op jit(solution)/shard_map/all_to_all | solution.py:18
  25.6 2.0 fusion.62
  36.3 1.3 fusion.33
  37.6 13.9 %all-to-all-done = bf16[4,384,768]{1,2,0:T(8,128)(2,1)} async-done(((bf16[4,384,768]{1,2,0:T(8,128)(2,1)}), bf16[4,384,768]{1,2,0:T(8,128)(2,1)}, u32[]{:S(2)}, u32[]{:S(2)}) %all-to-all-start) | async-done | bytes 2359328 | tf_op jit(solution)/shard_map/all_to_all | solution.py:18
  51.5 21.0 %all-gather.3.cloned.1.call-done = bf16[1,384,3072]{2,1,0:T(8,128)(2,1)} async-done(((bf16[1,384,384]{2,1,0:T(8,128)(2,1)}), bf16[1,384,3072]{2,1,0:T(8,128)(2,1)}) %all-gather.3.cloned.1.call-update) | async-done | bytes 2359312 | tf_op jit(solution)/shard_map/all_gather | solution.py:111
  72.5 4.0 %fusion.22 = bf16[384,384]{0,1:T(8,128)(2,1)S(1)} fusion(bf16[384,3072]{0,1:T(8,128)(2,1)} %bitcast.12, bf16[1,384,3072]{2,1,0:T(8,128)(2,1)} %all-gather.3.cloned.1.call-done, f32[3072]{0:T(1024)S(1)} %bitcast.122), kind=kOutput, calls=%fused_computation.38 | convolution fusion | flops 909656064 | bytes 5025792 | tf_op jit(solution)/shard_map/dot_general | solution.py:115
  81.1 1.6 fusion.11
  82.9 1.6 fusion.12
  84.5 2.2 convolution_multiply_fusion.3
  86.7 1.4 convolution_convert_fusion
  88.1 2.5 %copy.29 = bf16[384,3072]{0,1:T(8,128)(2,1)} copy(bf16[384,3072]{1,0:T(8,128)(2,1)S(1)} %convolution_convert_fusion) | data formatting | bytes 4718592 | tf_op jit(solution)/shard_map/convert_element_type | solution.py:165
  90.6 7.7 %all-to-all-start.1 = ((bf16[32,384,96]{1,2,0:T(8,128)(2,1)}), bf16[32,384,96]{1,2,0:T(8,128)(2,1)S(1)}, u32[]{:S(2)}, u32[]{:S(2)}) async-start(bf16[32,384,96]{1,2,0:T(8,128)(2,1)} %bitcast.112), calls=%async_computation.1 | async-start | bytes 4718592 | tf_op jit(solution)/shard_map/all_to_all | solution.py:56
  98.3 1.5 fusion.76
  103.5 3.4 %collective-permute-start.3 = (bf16[2,384,384]{1,2,0:T(8,128)(2,1)}, bf16[2,384,384]{1,2,0:T(8,128)(2,1)}, u32[]{:S(2)}, u32[]{:S(2)}) collective-permute-start(bf16[2,384,384]{1,2,0:T(8,128)(2,1)} %pad_maximum_fusion.4), channel_id=1, source_target_pairs={{0,8},{8,16},{16,24},{24,32},{32,40},{40,48},{48,56},{1,9},{9,17},... | collective-permute-start | bytes 1769480 | tf_op jit(solution)/shard_map/ppermute | solution.py:45
  107.8 3.3 %collective-permute-start.2 = (bf16[2,384,384]{1,2,0:T(8,128)(2,1)}, bf16[2,384,384]{1,2,0:T(8,128)(2,1)}, u32[]{:S(2)}, u32[]{:S(2)}) collective-permute-start(bf16[2,384,384]{1,2,0:T(8,128)(2,1)} %pad_maximum_fusion.3), channel_id=1, source_target_pairs={{8,0},{16,8},{24,16},{32,24},{40,32},{48,40},{56,48},{9,1},{17,9},... | collective-permute-start | bytes 1769480 | tf_op jit(solution)/shard_map/ppermute | solution.py:45
  112.5 1.8 fusion.28
  114.3 1.5 pad_maximum_fusion.1
  115.8 14.6 %all-to-all-done.1 = bf16[32,384,96]{1,2,0:T(8,128)(2,1)S(1)} async-done(((bf16[32,384,96]{1,2,0:T(8,128)(2,1)}), bf16[32,384,96]{1,2,0:T(8,128)(2,1)S(1)}, u32[]{:S(2)}, u32[]{:S(2)}) %all-to-all-start.1) | async-done | bytes 2359328 | tf_op jit(solution)/shard_map/all_to_all | solution.py:56
  131.8 6.2 %all-to-all-start.2 = ((f32[8,384,96]{1,2,0:T(8,128)}), f32[8,384,96]{1,2,0:T(8,128)S(1)}, u32[]{:S(2)}, u32[]{:S(2)}) async-start(f32[8,384,96]{1,2,0:T(8,128)} %broadcast_in_dim.64), calls=%async_computation.2 | async-start | bytes 2359296 | tf_op jit(solution)/shard_map/all_to_all | solution.py:18
  138.0 1.9 fusion.29
  139.9 1.7 fusion.30
  142.3 1.8 copy.30
  144.2 1.5 pad_maximum_fusion
  145.7 61.4 %all-reduce.3.cloned.1.call-done = (bf16[1,256,384]{1,2,0:T(8,128)(2,1)}, bf16[1,256,384]{1,2,0:T(8,128)(2,1)}) async-done(((bf16[1,256,384]{1,2,0:T(8,128)(2,1)}, bf16[1,256,384]{1,2,0:T(8,128)(2,1)}), (bf16[1,256,384]{1,2,0:T(8,128)(2,1)}, bf16[1,256,384]{1,2,0:T(8,128)(2,1)})) %all-reduce.3.cloned.1.call-update) | async-done | bytes 393232 | tf_op jit(solution)/shard_map/psum | solution.py:159
  207.1 1.7 copy.33
  208.9 1.7 copy.34
  212.9 1.5 fusion.41
  216.2 1.4 copy.35
  (137 shorter events, 29.4 us)
Async XLA Ops:
  9.2 18.7 %collective-permute-start.1 = (bf16[2,384,384]{2,1,0:T(8,128)(2,1)S(1)}, bf16[2,384,384]{2,1,0:T(8,128)(2,1)S(1)}, u32[]{:S(2)}, u32[]{:S(2)}) collective-permute-start(bf16[2,384,384]{2,1,0:T(8,128)(2,1)S(1)} %constant_dynamic-update-slice_fusion), channel_id=1, source_target_pairs={{8,0},{16,8},{24,16},{32,24},{40,32},{48,40},{56,48},{9,1},{17,9},... | collective-permute-start | bytes 1769480 | tf_op jit(solution)/shard_map/ppermute | solution.py:35
  13.3 14.7 %collective-permute-start = (bf16[2,384,384]{2,1,0:T(8,128)(2,1)S(1)}, bf16[2,384,384]{2,1,0:T(8,128)(2,1)S(1)}, u32[]{:S(2)}, u32[]{:S(2)}) collective-permute-start(bf16[2,384,384]{2,1,0:T(8,128)(2,1)S(1)} %constant_dynamic-update-slice_fusion), channel_id=1, source_target_pairs={{0,8},{8,16},{16,24},{24,32},{32,40},{40,48},{48,56},{1,9},{9,17},... | collective-permute-start | bytes 1769480 | tf_op jit(solution)/shard_map/ppermute | solution.py:33
  18.3 6.1 %copy-start.36 = (s32[1,2]{1,0:T(1,128)S(1)}, s32[1,2]{1,0:T(1,128)}, u32[]{:S(2)}) copy-start(s32[1,2]{1,0:T(1,128)} %param.19) | copy-start | bytes 28
  18.3 6.7 %copy-start.38 = (s32[8,1]{0,1:T(1,128)S(1)}, s32[8,1]{0,1:T(1,128)}, u32[]{:S(2)}) copy-start(s32[8,1]{0,1:T(1,128)} %param.20) | copy-start | bytes 100
  18.3 9.3 %copy-start.35 = (bf16[1,3072]{1,0:T(2,128)(2,1)S(1)}, bf16[1,3072]{1,0:T(2,128)(2,1)}, u32[]{:S(2)}) copy-start(bf16[1,3072]{1,0:T(2,128)(2,1)} %param.17) | copy-start | bytes 18436
  18.3 9.5 %copy-start.29 = (bf16[1,256,384]{2,1,0:T(8,128)(2,1)S(1)}, bf16[1,256,384]{2,1,0:T(8,128)(2,1)}, u32[]{:S(2)}) copy-start(bf16[1,256,384]{2,1,0:T(8,128)(2,1)} %param.14) | copy-start | bytes 589828
  18.3 9.5 %copy-start.30 = (bf16[1,256,384]{2,1,0:T(8,128)(2,1)S(1)}, bf16[1,256,384]{2,1,0:T(8,128)(2,1)}, u32[]{:S(2)}) copy-start(bf16[1,256,384]{2,1,0:T(8,128)(2,1)} %param.15) | copy-start | bytes 589828
  18.3 33.2 %all-to-all-start = ((bf16[4,384,768]{1,2,0:T(8,128)(2,1)}), bf16[4,384,768]{1,2,0:T(8,128)(2,1)}, u32[]{:S(2)}, u32[]{:S(2)}) async-start(bf16[4,384,768]{1,2,0:T(8,128)(2,1)} %broadcast_in_dim.59), calls=%async_computation | async-start | bytes 4718592 | tf_op jit(solution)/shard_map/all_to_all | solution.py:18
  23.0 49.5 %all-gather.3.cloned.1.call-start = ((), (), s32[]{:S(2)}) async-start(), calls=%async_computation.3 | async-start | bytes 2654208 | tf_op jit(solution)/shard_map/all_gather | solution.py:111
  27.8 2.6 %copy-start.32 = (bf16[256,128]{1,0:T(8,128)(2,1)}, bf16[256,128]{1,0:T(8,128)(2,1)S(1)}, u32[]{:S(2)}) copy-start(bf16[256,128]{1,0:T(8,128)(2,1)S(1)} %get-tuple-element.40) | copy-start | bytes 196612
  27.9 6.3 %copy-start.33 = (bf16[256,128]{1,0:T(8,128)(2,1)}, bf16[256,128]{1,0:T(8,128)(2,1)S(1)}, u32[]{:S(2)}) copy-start(bf16[256,128]{1,0:T(8,128)(2,1)S(1)} %get-tuple-element.37) | copy-start | bytes 196612
  29.5 1.9 copy-start.20
  29.5 3.3 %copy-start.23 = (bf16[1152,128]{1,0:T(8,128)(2,1)}, bf16[1152,128]{1,0:T(8,128)(2,1)S(1)}, u32[]{:S(2)}) copy-start(bf16[1152,128]{1,0:T(8,128)(2,1)S(1)} %get-tuple-element.32) | copy-start | bytes 884740
  29.5 4.7 %copy-start.25 = (bf16[1152,128]{1,0:T(8,128)(2,1)}, bf16[1152,128]{1,0:T(8,128)(2,1)S(1)}, u32[]{:S(2)}) copy-start(bf16[1152,128]{1,0:T(8,128)(2,1)S(1)} %get-tuple-element.31) | copy-start | bytes 884740
  31.0 2.8 %copy-start.2 = (f32[384,1408]{0,1:T(8,128)}, f32[384,1408]{0,1:T(8,128)S(1)}, u32[]{:S(2)}) copy-start(f32[384,1408]{0,1:T(8,128)S(1)} %get-tuple-element.50) | copy-start | bytes 6488068
  31.9 4.3 %copy-start = (f32[384,1408]{0,1:T(8,128)}, f32[384,1408]{0,1:T(8,128)S(1)}, u32[]{:S(2)}) copy-start(f32[384,1408]{0,1:T(8,128)S(1)} %get-tuple-element.46) | copy-start | bytes 6488068
  72.5 4.0 %copy-start.16 = (bf16[384,1408]{0,1:T(8,128)(2,1)S(1)}, bf16[384,1408]{0,1:T(8,128)(2,1)}, u32[]{:S(2)}) copy-start(bf16[384,1408]{0,1:T(8,128)(2,1)} %copy-done.15) | copy-start | bytes 3244036
  72.5 4.4 %copy-start.14 = (bf16[384,1408]{0,1:T(8,128)(2,1)S(1)}, bf16[384,1408]{0,1:T(8,128)(2,1)}, u32[]{:S(2)}) copy-start(bf16[384,1408]{0,1:T(8,128)(2,1)} %copy-done.13) | copy-start | bytes 3244036
  76.9 2.6 %copy-start.22 = (bf16[1152,128]{1,0:T(8,128)(2,1)S(1)}, bf16[1152,128]{1,0:T(8,128)(2,1)}, u32[]{:S(2)}) copy-start(bf16[1152,128]{1,0:T(8,128)(2,1)} %get-tuple-element.33) | copy-start | bytes 884740
  76.9 2.6 %copy-start.39 = (bf16[384,128]{0,1:T(8,128)(2,1)S(1)}, bf16[384,128]{0,1:T(8,128)(2,1)}, u32[]{:S(2)}) copy-start(bf16[384,128]{0,1:T(8,128)(2,1)} %convolution_convert_fusion.2) | copy-start | bytes 294916
  76.9 2.6 %copy-start.40 = (bf16[384,128]{0,1:T(8,128)(2,1)S(1)}, bf16[384,128]{0,1:T(8,128)(2,1)}, u32[]{:S(2)}) copy-start(bf16[384,128]{0,1:T(8,128)(2,1)} %convolution_convert_fusion.1) | copy-start | bytes 294916
  78.3 1.9 copy-start.34
  80.7 3.8 %copy-start.19 = (bf16[384,1408]{0,1:T(8,128)(2,1)}, bf16[384,1408]{0,1:T(8,128)(2,1)S(1)}, u32[]{:S(2)}) copy-start(bf16[384,1408]{0,1:T(8,128)(2,1)S(1)} %fusion.10) | copy-start | bytes 3244036
  82.9 3.8 %copy-start.37 = (bf16[1,384,3072]{2,1,0:T(8,128)(2,1)S(1)}, bf16[1,384,3072]{2,1,0:T(8,128)(2,1)}, u32[]{:S(2)}) copy-start(bf16[1,384,3072]{2,1,0:T(8,128)(2,1)} %all-gather.3.cloned.1.call-done) | copy-start | bytes 7077892
  90.6 39.8 %all-to-all-start.1 = ((bf16[32,384,96]{1,2,0:T(8,128)(2,1)}), bf16[32,384,96]{1,2,0:T(8,128)(2,1)S(1)}, u32[]{:S(2)}, u32[]{:S(2)}) async-start(bf16[32,384,96]{1,2,0:T(8,128)(2,1)} %bitcast.112), calls=%async_computation.1 | async-start | bytes 4718592 | tf_op jit(solution)/shard_map/all_to_all | solution.py:56
  98.3 108.9 %all-reduce.3.cloned.1.call-start = ((), (), s32[]{:S(2)}) async-start(), calls=%async_computation.4 | async-start | bytes 786432 | tf_op jit(solution)/shard_map/psum | solution.py:159
  103.5 107.1 %collective-permute-start.3 = (bf16[2,384,384]{1,2,0:T(8,128)(2,1)}, bf16[2,384,384]{1,2,0:T(8,128)(2,1)}, u32[]{:S(2)}, u32[]{:S(2)}) collective-permute-start(bf16[2,384,384]{1,2,0:T(8,128)(2,1)} %pad_maximum_fusion.4), channel_id=1, source_target_pairs={{0,8},{8,16},{16,24},{24,32},{32,40},{40,48},{48,56},{1,9},{9,17},... | collective-permute-start | bytes 1769480 | tf_op jit(solution)/shard_map/ppermute | solution.py:45
  107.8 104.0 %collective-permute-start.2 = (bf16[2,384,384]{1,2,0:T(8,128)(2,1)}, bf16[2,384,384]{1,2,0:T(8,128)(2,1)}, u32[]{:S(2)}, u32[]{:S(2)}) collective-permute-start(bf16[2,384,384]{1,2,0:T(8,128)(2,1)} %pad_maximum_fusion.3), channel_id=1, source_target_pairs={{8,0},{16,8},{24,16},{32,24},{40,32},{48,40},{56,48},{9,1},{17,9},... | collective-permute-start | bytes 1769480 | tf_op jit(solution)/shard_map/ppermute | solution.py:45
  131.8 84.4 %all-to-all-start.2 = ((f32[8,384,96]{1,2,0:T(8,128)}), f32[8,384,96]{1,2,0:T(8,128)S(1)}, u32[]{:S(2)}, u32[]{:S(2)}) async-start(f32[8,384,96]{1,2,0:T(8,128)} %broadcast_in_dim.64), calls=%async_computation.2 | async-start | bytes 2359296 | tf_op jit(solution)/shard_map/all_to_all | solution.py:18
  138.0 6.2 %copy-start.7 = (f32[1408,128]{0,1:T(8,128)S(1)}, f32[1408,128]{0,1:T(8,128)}, u32[]{:S(2)}) copy-start(f32[1408,128]{0,1:T(8,128)} %convolution_multiply_fusion.3) | copy-start | bytes 2162692
  138.0 6.2 %copy-start.9 = (f32[1408,128]{0,1:T(8,128)S(1)}, f32[1408,128]{0,1:T(8,128)}, u32[]{:S(2)}) copy-start(f32[1408,128]{0,1:T(8,128)} %copy-done.8) | copy-start | bytes 2162692
  138.0 6.2 %copy-start.11 = (f32[1408,128]{0,1:T(8,128)S(1)}, f32[1408,128]{0,1:T(8,128)}, u32[]{:S(2)}) copy-start(f32[1408,128]{0,1:T(8,128)} %copy-done.10) | copy-start | bytes 2162692
  (18 other events, 26.6 us)
Sparse Core Ops, SparseCore 0:
  25.6 46.8 all-gather.2
  112.6 94.5 all-reduce.2
where the time goes:
time: 229 us; the launch traced here: 224 us
  waiting for transfers between devices  112 us (49%)
  starting transfers between devices  31.2 us (14%)
  matrix products  24.9 us (11%)
  local copies, waits for them, and re-layouts  24.4 us (11%)
  other arithmetic  16.9 us (7%)
  between operations  15.2 us (7%)
    psum x1, waiting for transfers between devices, per_device(): lax.psum(grad_k[3 * tok:].astype(jnp.bfloat16), 'sp').astype(jnp.float32)  61.4 us
    all_gather x1, waiting for transfers between devices, per_device(): full_grad = lax.all_gather(grad_out[0], 'tp', axis=1, tiled=True)  21 us
    all_to_all x1, waiting for transfers between devices, summed_on_arrival(): parts = lax.all_to_all(cut_along(shard, dim, count), axis, 0, 0, tiled=True)  14.6 us
    unnamed x90, local copies, waits for them, and re-layouts  14.1 us
    all_to_all x2, waiting for transfers between devices, from_everyone(): return lax.all_to_all(copies, axis, split_axis=0, concat_axis=0, tiled=True)  13.9 us
    all_to_all x2, starting transfers between devices, from_everyone(): return lax.all_to_all(copies, axis, split_axis=0, concat_axis=0, tiled=True)  10.8 us
    all_to_all x1, starting transfers between devices, summed_on_arrival(): parts = lax.all_to_all(cut_along(shard, dim, count), axis, 0, 0, tiled=True)  7.66 us
    ppermute x2, starting transfers between devices, shifted(): return lax.ppermute(block, axis, route)  6.63 us
  transfers between devices with their start and end apart: 9, of which 5 were waited for; matrix products, arithmetic and copies ran while one was open for 19% of the time, Pallas kernels for 0%

commit v1 on v0

v1 whole, which is shorter than its diff:
```python
import jax
import jax.numpy as jnp
from jax import lax
from jax.experimental import pallas as pl
from jax.experimental.pallas import tpu as pltpu
from jax.sharding import Mesh, PartitionSpec as P

HD = 128
B16 = jnp.bfloat16
F32 = jnp.float32
NEG = -1e30
LOG2E = 1.4426950408889634

VM = pltpu.MemorySpace.VMEM
SM = pltpu.MemorySpace.SMEM


def vspec():
    return pl.BlockSpec(memory_space=VM)


def sspec():
    return pl.BlockSpec(memory_space=SM)


def nn(a, b):
    return lax.dot_general(a, b, (((1,), (0,)), ((), ())), preferred_element_type=F32)


def nt(a, b):
    return lax.dot_general(a, b, (((1,), (1,)), ((), ())), preferred_element_type=F32)


def ring(count, step):
    return [(i, (i + step) % count) for i in range(count)]


def forward_kernel(flags, q, kown, vown, prev, nxt, tk, tv, probs, att_t):
    tok, width = q.shape
    txt = tk.shape[0]
    factor = HD ** (-0.5) * LOG2E
    for h in range(width // HD):
        cols = slice(h * HD, (h + 1) * HD)
        qh = q[:, cols]
        keys = [prev[0, :, cols], kown[:, cols], nxt[0, :, cols]]
        scores = []
        for place in range(3):
            s = nt(keys[place], qh)
            scores.append(jnp.where(flags[place] != 0, s, NEG))
        s = nt(tk[:, cols], qh)
        live = lax.broadcasted_iota(jnp.int32, (txt, tok), 0) < flags[3]
        scores.append(jnp.where(live, s, NEG))
        top = scores[0].max(axis=0, keepdims=True)
        for s in scores[1:]:
            top = jnp.maximum(top, s.max(axis=0, keepdims=True))
        shift = top * factor
        total = jnp.zeros((1, tok), F32)
        expd = []
        for s in scores:
            e = jnp.exp2(s * factor - shift)
            total = total + e.sum(axis=0, keepdims=True)
            expd.append(e)
        inverse = 1.0 / total
        values = [prev[1, :, cols], vown[:, cols], nxt[1, :, cols], tv[:, cols]]
        out = jnp.zeros((HD, tok), F32)
        row = 0
        for e, v in zip(expd, values):
            p = (e * inverse).astype(B16)
            probs[h, row : row + p.shape[0], :] = p
            row += p.shape[0]
            out = out + nn(v.T, p)
        att_t[cols, :] = out.astype(B16)


def forward(flags, q, kown, vown, prev, nxt, tk, tv):
    tok, width = q.shape
    keys = 3 * tok + tk.shape[0]
    return pl.pallas_call(
        forward_kernel,
        out_shape=(
            jax.ShapeDtypeStruct((width // HD, keys, tok), B16),
            jax.ShapeDtypeStruct((width, tok), B16),
        ),
        in_specs=[sspec()] + [vspec()] * 7,
        out_specs=(vspec(), vspec()),
        name="attn_fwd",
    )(flags, q, kown, vown, prev, nxt, tk, tv)


def contract_shard(flags, block, shard, gate, w_near, w_far, att_t, lw):
    side = block & 1
    owner = block >> 1
    diff = owner ^ flags[5]
    across = diff >> 1
    scaled = (shard.astype(F32) * gate[block].astype(F32)).astype(B16)
    w = jnp.where((diff & 1) == 0, w_near[across, side], w_far[across, side])
    part = nn(att_t, scaled).astype(B16)
    lw[diff & 1, owner >> 1, side] = part
    return nt(w, scaled)


def early_kernel(flags, s0, s1, s2, s3, s4, gate, w_near, w_far, att, acc, lw):
    t = flags[4]
    att_t = att[...]
    total = None
    for step, ref in ((0, s0), (7, s1), (1, s2), (6, s3), (2, s4)):
        part = contract_shard(flags, (t + step) & 7, ref[...], gate, w_near, w_far, att_t, lw)
        total = part if total is None else total + part
    acc[...] = total


def late_kernel(flags, s5, s6, s7a, s7b, gate, w_near, w_far, att, acc, lw_in, ga, lw):
    lw[...] = lw_in[...]
    t = flags[4]
    att_t = att[...]
    total = acc[...]
    total = total + contract_shard(flags, (t + 5) & 7, s5[...], gate, w_near, w_far, att_t, lw)
    total = total + contract_shard(flags, (t + 3) & 7, s6[...], gate, w_near, w_far, att_t, lw)
    both = jnp.concatenate([s7a[...], s7b[...]], axis=0)
    total = total + contract_shard(flags, (t + 4) & 7, both, gate, w_near, w_far, att_t, lw)
    ga[...] = total.astype(B16)


def early(flags, shards, gate, w_near, w_far, att_t):
    tok = shards[0].shape[0]
    width = att_t.shape[0]
    return pl.pallas_call(
        early_kernel,
        out_shape=(
            jax.ShapeDtypeStruct((width, tok), F32),
            jax.ShapeDtypeStruct((2, 2, 2, width, shards[0].shape[1]), B16),
        ),
        in_specs=[sspec()] + [vspec()] * 9,
        out_specs=(vspec(), vspec()),
        name="contract_early",
    )(flags, *shards, gate, w_near, w_far, att_t)


def late(flags, shards, gate, w_near, w_far, att_t, acc, lw):
    tok = shards[0].shape[0]
    width = att_t.shape[0]
    return pl.pallas_call(
        late_kernel,
        out_shape=(
            jax.ShapeDtypeStruct((width, tok), B16),
            jax.ShapeDtypeStruct(lw.shape, lw.dtype),
        ),
        in_specs=[sspec()] + [vspec()] * 10,
        out_specs=(vspec(), vspec()),
        input_output_aliases={10: 1},
        name="contract_late",
    )(flags, *shards, gate, w_near, w_far, att_t, acc, lw)


def piece_grads(p_t, key, value, qh, ga_t, ga, delta):
    grad_p = nn(value, ga_t)
    ds_t = (p_t.astype(F32) * (grad_p - delta)).astype(B16)
    factor = HD ** (-0.5)
    return ds_t, factor * nn(ds_t, qh), nn(p_t, ga)


def backward_kernel(
    q, kown, vown, prev, nxt, tk, tv, probs, att, gat, gq, gprev, gown, gnext, gtext
):
    tok, width = q.shape
    factor = HD ** (-0.5)
    for h in range(width // HD):
        cols = slice(h * HD, (h + 1) * HD)
        qh = q[:, cols]
        ga_t = gat[cols, :]
        ga = ga_t.T
        delta = jnp.sum(ga_t.astype(F32) * att[cols, :].astype(F32), axis=0, keepdims=True)
        pieces = (
            (3 * tok, tk[:, cols], tv[:, cols], gtext),
            (0, prev[0, :, cols], prev[1, :, cols], gprev),
            (2 * tok, nxt[0, :, cols], nxt[1, :, cols], gnext),
            (tok, kown[:, cols], vown[:, cols], gown),
        )
        gq_t = jnp.zeros((HD, tok), F32)
        for row, key, value, out in pieces:
            p_t = probs[h, row : row + key.shape[0], :]
            ds_t, gk, gv = piece_grads(p_t, key, value, qh, ga_t, ga, delta)
            out[0, :, cols] = gk.astype(out.dtype)
            out[1, :, cols] = gv.astype(out.dtype)
            gq_t = gq_t + nn(key.T, ds_t)
        gq[:, cols] = (factor * gq_t).T.astype(B16)


def backward(q, kown, vown, prev, nxt, tk, tv, probs, att_t, ga_t):
    tok, width = q.shape
    txt = tk.shape[0]
    return pl.pallas_call(
        backward_kernel,
        out_shape=(
            jax.ShapeDtypeStruct((tok, width), B16),
            jax.ShapeDtypeStruct((2, tok, width), B16),
            jax.ShapeDtypeStruct((2, tok, width), F32),
            jax.ShapeDtypeStruct((2, tok, width), B16),
            jax.ShapeDtypeStruct((2, txt, width), B16),
        ),
        in_specs=[vspec()] * 10,
        out_specs=(vspec(),) * 5,
        name="attn_bwd",
    )(q, kown, vown, prev, nxt, tk, tv, probs, att_t, ga_t)


def visibility(windows, tile_map, text_count, index, slabs):
    padded = jnp.concatenate([tile_map[:1], tile_map, tile_map[:1]], axis=0)
    side = lax.dynamic_slice_in_dim(padded, index, 3, 0)[:, 0]
    own = side[1]
    offset = jnp.arange(3, dtype=jnp.int32) - 1
    others = index + offset
    allowed = (
        (jnp.abs(offset) <= windows[0, 0])
        & (jnp.abs(own - side) <= windows[0, 1])
        & (others >= 0)
        & (others < slabs)
    )
    return allowed.astype(jnp.int32)


def per_device(
    query, key, value, text_key, text_value, grad_out, gate, out_weight, windows, tile_map, text_count
):
    sp = lax.axis_size("sp")
    tp = lax.axis_size("tp")
    tok, width = query.shape[1], query.shape[2]
    txt = text_key.shape[1]
    rows = out_weight.shape[0]
    index = lax.axis_index("sp")
    dp_index = lax.axis_index("dy") * 2 + lax.axis_index("dc")
    flags = jnp.concatenate(
        [
            visibility(windows, tile_map, text_count, index, sp),
            text_count,
            lax.axis_index("tp")[None],
            dp_index[None],
        ]
    ).astype(jnp.int32)

    own = grad_out[0]
    right = [own]
    left = [own]
    for _ in range(3):
        right.append(lax.ppermute(right[-1], "tp", ring(tp, 1)))
        left.append(lax.ppermute(left[-1], "tp", ring(tp, -1)))
    half = tok // 2
    last_a = lax.ppermute(right[3][:half], "tp", ring(tp, 1))
    last_b = lax.ppermute(left[3][half:], "tp", ring(tp, -1))

    pair = jnp.stack([key[0], value[0]], axis=0)
    prev = lax.ppermute(pair, "sp", [(i, i + 1) for i in range(sp - 1)])
    nxt = lax.ppermute(pair, "sp", [(i + 1, i) for i in range(sp - 1)])

    w_own = jnp.swapaxes(out_weight.reshape(rows, 2, -1), 0, 1)
    w_across = lax.ppermute(w_own, "dy", [(0, 1), (1, 0)])
    w_near = jnp.stack([w_own, w_across], axis=0)
    w_far = lax.ppermute(w_near, "dc", [(0, 1), (1, 0)])
    gates = gate[0].reshape(tp, 1, -1)

    q, k, v, tk, tv = query[0], key[0], value[0], text_key[0], text_value[0]
    probs, att_t = forward(flags, q, k, v, prev, nxt, tk, tv)
    acc, lw = early(
        flags, (own, right[1], left[1], right[2], left[2]), gates, w_near, w_far, att_t
    )
    ga_t, lw = late(
        flags, (right[3], left[3], last_a, last_b), gates, w_near, w_far, att_t, acc, lw
    )

    other = lax.ppermute(lw[1], "dc", [(0, 1), (1, 0)])
    lw2 = (lw[0].astype(F32) + other.astype(F32)).astype(B16)
    cut = rows // sp
    lw2 = lw2.reshape(2, 2, sp, cut, -1)
    lw2 = jnp.transpose(lw2, (0, 2, 1, 3, 4)).reshape(2 * sp, 2, cut, -1)
    lw_in = lax.all_to_all(lw2, ("dy", "sp"), 0, 0, tiled=True)
    lw_sum = jnp.sum(lw_in.astype(F32), axis=0).astype(B16)

    gq, gprev, gown, gnext, gtext = backward(q, k, v, prev, nxt, tk, tv, probs, att_t, ga_t)

    tcut = txt // sp
    text_parts = jnp.swapaxes(gtext.reshape(2, sp, tcut, width), 0, 1)
    text_in = lax.all_to_all(text_parts, "sp", 0, 0, tiled=True)
    text_sum = jnp.sum(text_in.astype(F32), axis=0).astype(B16)

    from_later = lax.ppermute(gprev, "sp", [(i + 1, i) for i in range(sp - 1)])
    from_earlier = lax.ppermute(gnext, "sp", [(i, i + 1) for i in range(sp - 1)])
    total = (gown + from_later.astype(F32) + from_earlier.astype(F32)).astype(B16)

    mine = jnp.concatenate(
        [lw_sum.reshape(2 * cut, width), text_sum.reshape(2 * tcut, width)], axis=0
    )
    copies = jnp.broadcast_to(mine[None], (sp, *mine.shape))
    gathered = lax.all_to_all(copies, "sp", 0, 0, tiled=True)
    weight = gathered[:, : 2 * cut].reshape(sp, 2, cut, width)
    weight = jnp.transpose(weight, (0, 2, 1, 3)).reshape(rows, 2 * width).astype(F32)
    text = gathered[:, 2 * cut :].reshape(sp, 2, tcut, width)
    text_k = text[:, 0].reshape(txt, width)
    text_v = text[:, 1].reshape(txt, width)
    return (
        gq[None],
        total[0][None],
        total[1][None],
        text_k[None],
        text_v[None],
        weight,
    )


def solution(mesh):
    shape = mesh.devices.shape
    fine = Mesh(mesh.devices.reshape(2, shape[0] // 2, *shape[1:]), ("dy", "dc", "sp", "tp"))
    dp = ("dy", "dc")
    placed = (
        P(dp, "sp", "tp"),
        P(dp, "sp", "tp"),
        P(dp, "sp", "tp"),
        P(dp, None, "tp"),
        P(dp, None, "tp"),
        P(dp, "sp", "tp"),
        P(dp, None),
        P("tp", dp),
        P("sp", None),
        P(),
        P(dp),
    )
    return jax.shard_map(
        per_device,
        mesh=fine,
        in_specs=placed,
        out_specs=(
            P(dp, "sp", "tp"),
            P(dp, "sp", "tp"),
            P(dp, "sp", "tp"),
            P(dp, None, "tp"),
            P(dp, None, "tp"),
            P("tp", dp),
        ),
        check_vma=False,
    )
```

time: 229 us -> 159 us (0.69); the launches traced: 224 us -> 158 us
  waiting for transfers between devices: 112 us -> 56.1 us
  Pallas kernels: 0 us -> 26 us
  matrix products: 24.9 us -> 0 us
  starting transfers between devices: 31.2 us -> 48.1 us
  between operations: 15.2 us -> 1.49 us
  other arithmetic: 16.9 us -> 6.05 us
  local copies, waits for them, and re-layouts: 24.4 us -> 20.1 us
    psum x1 -> x0, waiting for transfers between devices: 61.4 us -> none  [per_device(): lax.psum(grad_k[3 * tok:].astype(jnp.bfloat16), 'sp').astype(jnp.float32)]
    ppermute x4 -> x15, waiting for transfers between devices: 0.16 us -> 29.5 us  [the longest x1 13.5 us: per_device(): w_across = lax.ppermute(w_own, 'dy', [(0, 1), (1, 0)])]
    pallas_call x0 -> x4, Pallas kernels: none -> 26 us  [the longest x1 8.1 us: backward(): pl.pallas_call(backward_kernel, out_shape=(jax.ShapeDtypeStruct((tok, wid...]
    dot_general x20 -> x0, matrix products: 24.9 us -> none  [the longest x3 5.35 us: tile_attention(): jnp.dot(grad_scores, keys, preferred_element_type=jnp.float32)]
    all_gather x1 -> x0, waiting for transfers between devices: 21 us -> none  [per_device(): full_grad = lax.all_gather(grad_out[0], 'tp', axis=1, tiled=True)]
    ppermute x4 -> x15, starting transfers between devices: 12.7 us -> 30 us  [the longest x3 13 us: per_device(): left.append(lax.ppermute(left[-1], 'tp', ring(tp, -1)))]
    unnamed x90 -> x29, local copies, waits for them, and re-layouts: 14.1 us -> 7.46 us
    another operation x4 -> x1, other arithmetic: 3.44 us -> 0.13 us  [per_device(): w_near = jnp.stack([w_own, w_across], axis=0)]
  transfers between devices with their start and end apart: 9 -> 18, of which waited for: 5 -> 8; matrix products, arithmetic and copies ran while one was open for 19% -> 9% of each run, Pallas kernels for 0% -> 13%
where the time goes in v1:
time: 159 us; the launch traced here: 158 us
  waiting for transfers between devices  56.1 us (35%)
  starting transfers between devices  48.1 us (30%)
  Pallas kernels  26 us (16%)
  local copies, waits for them, and re-layouts  20.1 us (13%)
  other arithmetic  6.05 us (4%)
    ppermute x1, waiting for transfers between devices, per_device(): w_across = lax.ppermute(w_own, 'dy', [(0, 1), (1, 0)])  13.5 us
    ppermute x3, starting transfers between devices, per_device(): left.append(lax.ppermute(left[-1], 'tp', ring(tp, -1)))  13 us
    all_to_all x1, waiting for transfers between devices, per_device(): lw_in = lax.all_to_all(lw2, ('dy', 'sp'), 0, 0, tiled=True)  12.7 us
    ppermute x3, waiting for transfers between devices, per_device(): left.append(lax.ppermute(left[-1], 'tp', ring(tp, -1)))  9.34 us
    all_to_all x1, starting transfers between devices, per_device(): text_in = lax.all_to_all(text_parts, 'sp', 0, 0, tiled=True)  8.19 us
    pallas_call x1, Pallas kernels, backward(): pl.pallas_call(backward_kernel, out_shape=(jax.ShapeDtypeStruct((tok, wid...  8.1 us
    unnamed x29, local copies, waits for them, and re-layouts  7.46 us
    all_to_all x1, waiting for transfers between devices, per_device(): text_in = lax.all_to_all(text_parts, 'sp', 0, 0, tiled=True)  6.97 us
  transfers between devices with their start and end apart: 18, of which 8 were waited for; matrix products, arithmetic and copies ran while one was open for 9% of the time, Pallas kernels for 13%

profile of v1, /device:TPU:2, one launch (start us, length us, event | category | flops | bytes accessed | tf_op | source)
XLA Modules:
  0.0 157.8 jit_solution(9283938719626013695)
XLA Ops:
  0.6 1.4 copy.25
  2.3 1.7 %collective-permute-start.10 = (bf16[2,384,384]{2,1,0:T(8,128)(2,1)S(1)}, bf16[2,384,384]{2,1,0:T(8,128)(2,1)S(1)}, u32[]{:S(2)}, u32[]{:S(2)}) collective-permute-start(bf16[2,384,384]{2,1,0:T(8,128)(2,1)S(1)} %bitcast.60), channel_id=1, source_target_pairs={{0,128},{128,0},{1,129},{129,1},{2,130},{130,2},{3,131},{131,3},{4... | collective-permute-start | bytes 1769480 | tf_op jit(solution)/shard_map/ppermute | solution.py:256
  4.0 13.5 %collective-permute-done.10 = bf16[2,384,384]{2,1,0:T(8,128)(2,1)S(1)} collective-permute-done((bf16[2,384,384]{2,1,0:T(8,128)(2,1)S(1)}, bf16[2,384,384]{2,1,0:T(8,128)(2,1)S(1)}, u32[]{:S(2)}, u32[]{:S(2)}) %collective-permute-start.10) | collective-permute-done | bytes 589856 | tf_op jit(solution)/shard_map/ppermute | solution.py:256
  18.4 5.9 %collective-permute-start.5 = (bf16[384,384]{1,0:T(8,128)(2,1)S(1)}, bf16[384,384]{1,0:T(8,128)(2,1)}, u32[]{:S(2)}, u32[]{:S(2)}) collective-permute-start(bf16[384,384]{1,0:T(8,128)(2,1)S(1)} %bitcast.73), channel_id=1, source_target_pairs={{0,7},{1,0},{2,1},{3,2},{4,3},{5,4},{6,5},{7,6},{8,15},{9,8},{10,9... | collective-permute-start | bytes 884744 | tf_op jit(solution)/shard_map/ppermute | solution.py:246
  24.3 6.2 %collective-permute-done.5.s2 = bf16[384,384]{1,0:T(8,128)(2,1)} collective-permute-done((bf16[384,384]{1,0:T(8,128)(2,1)S(1)}, bf16[384,384]{1,0:T(8,128)(2,1)}, u32[]{:S(2)}, u32[]{:S(2)}) %collective-permute-start.5) | collective-permute-done | bytes 294944 | tf_op jit(solution)/shard_map/ppermute | solution.py:246
  30.5 3.8 %collective-permute-start.6 = (bf16[384,384]{1,0:T(8,128)(2,1)}, bf16[384,384]{1,0:T(8,128)(2,1)}, u32[]{:S(2)}, u32[]{:S(2)}) collective-permute-start(bf16[384,384]{1,0:T(8,128)(2,1)} %collective-permute-done.5.s2), channel_id=1, source_target_pairs={{0,7},{1,0},{2,1},{3,2},{4,3},{5,4},{6,5},{7,6},{8,15},{9,8},{10,9... | collective-permute-start | bytes 884744 | tf_op jit(solution)/shard_map/ppermute | solution.py:246
  35.8 2.4 %collective-permute-start.1 = (bf16[2,384,384]{2,1,0:T(8,128)(2,1)}, bf16[2,384,384]{2,1,0:T(8,128)(2,1)S(1)}, u32[]{:S(2)}, u32[]{:S(2)}) collective-permute-start(bf16[2,384,384]{2,1,0:T(8,128)(2,1)} %constant_dynamic-update-slice_fusion), channel_id=1, source_target_pairs={{8,0},{16,8},{24,16},{32,24},{40,32},{48,40},{56,48},{9,1},{17,9},... | collective-permute-start | bytes 1769480 | tf_op jit(solution)/shard_map/ppermute | solution.py:253
  38.3 3.4 %collective-permute-start = (bf16[2,384,384]{2,1,0:T(8,128)(2,1)}, bf16[2,384,384]{2,1,0:T(8,128)(2,1)S(1)}, u32[]{:S(2)}, u32[]{:S(2)}) collective-permute-start(bf16[2,384,384]{2,1,0:T(8,128)(2,1)} %constant_dynamic-update-slice_fusion), channel_id=1, source_target_pairs={{0,8},{8,16},{16,24},{24,32},{32,40},{40,48},{48,56},{1,9},{9,17},... | collective-permute-start | bytes 1769480 | tf_op jit(solution)/shard_map/ppermute | solution.py:252
  41.7 3.3 %collective-permute-start.7 = (bf16[384,384]{1,0:T(8,128)(2,1)}, bf16[384,384]{1,0:T(8,128)(2,1)S(1)}, u32[]{:S(2)}, u32[]{:S(2)}) collective-permute-start(bf16[384,384]{1,0:T(8,128)(2,1)} %collective-permute-done.6.s4), channel_id=1, source_target_pairs={{0,7},{1,0},{2,1},{3,2},{4,3},{5,4},{6,5},{7,6},{8,15},{9,8},{10,9... | collective-permute-start | bytes 884744 | tf_op jit(solution)/shard_map/ppermute | solution.py:246
  46.5 3.1 %collective-permute-done.7.s6 = bf16[384,384]{1,0:T(8,128)(2,1)S(1)} collective-permute-done((bf16[384,384]{1,0:T(8,128)(2,1)}, bf16[384,384]{1,0:T(8,128)(2,1)S(1)}, u32[]{:S(2)}, u32[]{:S(2)}) %collective-permute-start.7) | collective-permute-done | bytes 294944 | tf_op jit(solution)/shard_map/ppermute | solution.py:246
  51.0 3.6 %collective-permute-start.9 = (bf16[192,384]{1,0:T(8,128)(2,1)}, bf16[192,384]{1,0:T(8,128)(2,1)}, u32[]{:S(2)}, u32[]{:S(2)}) collective-permute-start(bf16[192,384]{1,0:T(8,128)(2,1)} %slice.59), channel_id=1, source_target_pairs={{0,7},{1,0},{2,1},{3,2},{4,3},{5,4},{6,5},{7,6},{8,15},{9,8},{10,9... | collective-permute-start | bytes 442376 | tf_op jit(solution)/shard_map/ppermute | solution.py:249
  56.0 2.0 %fusion.3 = s32[3]{0:T(128)S(1)} fusion(s32[]{:T(128)S(6)} %axis_index.43, s32[]{:T(128)} %bitcast.7, s32[]{:T(128)} %bitcast.6, s32[]{:T(128)} %bitcast.5, s32[10,1]{0,1:T(1,128)S(1)} %pad_add_fusion, s32[]{:T(128)S(6)} %select_n.3), kind=kLoop, calls=%fused_computation.13 | loop fusion | flops 39 | bytes 44 | tf_op jit(solution)/shard_map/convert_element_type | solution.py:219
  60.4 6.5 %attn_fwd.1 = (bf16[3,1408,384]{2,1,0:T(8,128)(2,1)}, bf16[384,384]{1,0:T(8,128)(2,1)}) custom-call(s32[6]{0:T(128)} %pad_add_fusion.1.flags, bf16[384,384]{1,0:T(8,128)(2,1)} %bitcast.63, bf16[384,384]{1,0:T(8,128)(2,1)} %bitcast.54, bf16[384,384]{1,0:T(8,128)(2,1)} %bitcast.56, bf16[2,384,384]{2,1,0:T(8,128)(2,1)} %copy-done.6, ...), custom_call_target="tpu_custom_call" | custom-call | tf_op jit(solution)/shard_map/attn_fwd/pallas_call | solution.py:78
  68.0 5.6 %contract_early.1 = (f32[384,384]{1,0:T(8,128)}, bf16[2,2,2,384,384]{4,3,2,1,0:T(8,128)(2,1)}) custom-call(s32[6]{0:T(128)} %pad_add_fusion.1.flags, bf16[384,384]{1,0:T(8,128)(2,1)} %bitcast.72, bf16[384,384]{1,0:T(8,128)(2,1)} %collective-permute-done.2.s1, bf16[384,384]{1,0:T(8,128)(2,1)} %collective-permute-done.5.s2, ...), custom_call_target="tpu_custom_call" | custom-call | tf_op jit(solution)/shard_map/contract_early/pallas_call | solution.py:127
  73.6 5.8 %contract_late.1 = (bf16[384,384]{1,0:T(8,128)(2,1)}, bf16[2,2,2,384,384]{4,3,2,1,0:T(8,128)(2,1)}) custom-call(s32[6]{0:T(128)} %pad_add_fusion.1.flags, bf16[384,384]{1,0:T(8,128)(2,1)} %copy-done.9, bf16[384,384]{1,0:T(8,128)(2,1)} %copy-done.8, bf16[192,384]{1,0:T(8,128)(2,1)} %collective-permute-done.8.s7a, ...), custom_call_target="tpu_custom_call", output_to_operand_aliasing={{1}: (10, {})} | custom-call | tf_op jit(solution)/shard_map/contract_late/pallas_call | solution.py:142
  79.3 2.4 %slice_bitcast_fusion = bf16[2,2,384,384]{3,2,1,0:T(8,128)(2,1)} fusion(bf16[2,2,2,384,384]{4,3,2,1,0:T(8,128)(2,1)} %get-tuple-element.26), kind=kLoop, calls=%fused_computation.4 | loop fusion | bytes 2359296 | tf_op jit(solution)/shard_map/squeeze | solution.py:270
  81.8 8.1 %attn_bwd.1 = (bf16[384,384]{1,0:T(8,128)(2,1)}, bf16[2,384,384]{2,1,0:T(8,128)(2,1)}, f32[2,384,384]{2,1,0:T(8,128)}, bf16[2,384,384]{2,1,0:T(8,128)(2,1)}, bf16[2,256,384]{2,1,0:T(8,128)(2,1)}) custom-call(bf16[384,384]{1,0:T(8,128)(2,1)} %bitcast.64, bf16[384,384]{1,0:T(8,128)(2,1)} %bitcast.55, bf16[384,384]{1,0:T(8,128)(2,1)} %bitcast.57, ...), custom_call_target="tpu_custom_call" | custom-call | tf_op jit(solution)/shard_map/attn_bwd/pallas_call | solution.py:192
  89.9 1.8 %copy.32 = bf16[2,8,32,384]{3,2,0,1:T(8,128)(2,1)} copy(bf16[2,8,32,384]{3,2,1,0:T(8,128)(2,1)} %bitcast.71) | data formatting | bytes 786432 | tf_op jit(solution)/shard_map/reshape | solution.py:281
  91.7 8.2 %all-to-all-start.1 = ((bf16[8,2,32,384]{3,2,1,0:T(8,128)(2,1)}), bf16[8,2,32,384]{3,2,1,0:T(8,128)(2,1)S(1)}, u32[]{:S(2)}, u32[]{:S(2)}) async-start(bf16[8,2,32,384]{3,2,1,0:T(8,128)(2,1)} %bitcast.50), calls=%async_computation.1 | async-start | bytes 786432 | tf_op jit(solution)/shard_map/all_to_all | solution.py:282
  99.9 1.6 fusion
  101.5 1.2 copy.27
  102.6 7.0 %all-to-all-done.1 = bf16[8,2,32,384]{3,2,1,0:T(8,128)(2,1)S(1)} async-done(((bf16[8,2,32,384]{3,2,1,0:T(8,128)(2,1)}), bf16[8,2,32,384]{3,2,1,0:T(8,128)(2,1)S(1)}, u32[]{:S(2)}, u32[]{:S(2)}) %all-to-all-start.1) | async-done | bytes 393248 | tf_op jit(solution)/shard_map/all_to_all | solution.py:282
  109.6 4.7 %all-to-all-start = ((bf16[16,2,48,384]{3,2,1,0:T(8,128)(2,1)}), bf16[16,2,48,384]{3,2,1,0:T(8,128)(2,1)S(1)}, u32[]{:S(2)}, u32[]{:S(2)}) async-start(bf16[16,2,48,384]{3,2,1,0:T(8,128)(2,1)} %bitcast.22), calls=%async_computation | async-start | bytes 2359296 | tf_op jit(solution)/shard_map/all_to_all | solution.py:275
  114.3 2.1 %collective-permute-start.12 = (bf16[2,384,384]{2,1,0:T(8,128)(2,1)}, bf16[2,384,384]{2,1,0:T(8,128)(2,1)S(1)}, u32[]{:S(2)}, u32[]{:S(2)}) collective-permute-start(bf16[2,384,384]{2,1,0:T(8,128)(2,1)} %get-tuple-element.24), channel_id=1, source_target_pairs={{8,0},{16,8},{24,16},{32,24},{40,32},{48,40},{56,48},{9,1},{17,9},... | collective-permute-start | bytes 1769480 | tf_op jit(solution)/shard_map/ppermute | solution.py:285
  116.4 3.7 %collective-permute-start.13 = (bf16[2,384,384]{2,1,0:T(8,128)(2,1)}, bf16[2,384,384]{2,1,0:T(8,128)(2,1)}, u32[]{:S(2)}, u32[]{:S(2)}) collective-permute-start(bf16[2,384,384]{2,1,0:T(8,128)(2,1)} %get-tuple-element.25), channel_id=1, source_target_pairs={{0,8},{8,16},{16,24},{24,32},{32,40},{40,48},{48,56},{1,9},{9,17},... | collective-permute-start | bytes 1769480 | tf_op jit(solution)/shard_map/ppermute | solution.py:286
  120.2 12.7 %all-to-all-done = bf16[16,2,48,384]{3,2,1,0:T(8,128)(2,1)S(1)} async-done(((bf16[16,2,48,384]{3,2,1,0:T(8,128)(2,1)}), bf16[16,2,48,384]{3,2,1,0:T(8,128)(2,1)S(1)}, u32[]{:S(2)}, u32[]{:S(2)}) %all-to-all-start) | async-done | bytes 1179680 | tf_op jit(solution)/shard_map/all_to_all | solution.py:275
  134.2 5.3 %all-to-all-start.2 = ((bf16[8,160,384]{2,1,0:T(8,128)(2,1)}), bf16[8,160,384]{2,1,0:T(8,128)(2,1)S(1)}, u32[]{:S(2)}, u32[]{:S(2)}) async-start(bf16[8,160,384]{2,1,0:T(8,128)(2,1)} %broadcast_in_dim.18), calls=%async_computation.2 | async-start | bytes 1966080 | tf_op jit(solution)/shard_map/all_to_all | solution.py:293
  139.5 2.7 %collective-permute-done.12 = bf16[2,384,384]{2,1,0:T(8,128)(2,1)S(1)} collective-permute-done((bf16[2,384,384]{2,1,0:T(8,128)(2,1)}, bf16[2,384,384]{2,1,0:T(8,128)(2,1)S(1)}, u32[]{:S(2)}, u32[]{:S(2)}) %collective-permute-start.12) | collective-permute-done | bytes 589856 | tf_op jit(solution)/shard_map/ppermute | solution.py:285
  142.2 3.9 %collective-permute-done.13 = bf16[2,384,384]{2,1,0:T(8,128)(2,1)} collective-permute-done((bf16[2,384,384]{2,1,0:T(8,128)(2,1)}, bf16[2,384,384]{2,1,0:T(8,128)(2,1)}, u32[]{:S(2)}, u32[]{:S(2)}) %collective-permute-start.13) | collective-permute-done | bytes 589856 | tf_op jit(solution)/shard_map/ppermute | solution.py:286
  146.1 1.2 add_convert_fusion
  148.2 6.9 %all-to-all-done.2 = bf16[8,160,384]{2,1,0:T(8,128)(2,1)S(1)} async-done(((bf16[8,160,384]{2,1,0:T(8,128)(2,1)}), bf16[8,160,384]{2,1,0:T(8,128)(2,1)S(1)}, u32[]{:S(2)}, u32[]{:S(2)}) %all-to-all-start.2) | async-done | bytes 983072 | tf_op jit(solution)/shard_map/all_to_all | solution.py:293
  156.7 1.1 copy.30
  (63 shorter events, 13.5 us)
Async XLA Ops:
  2.3 15.2 %collective-permute-start.10 = (bf16[2,384,384]{2,1,0:T(8,128)(2,1)S(1)}, bf16[2,384,384]{2,1,0:T(8,128)(2,1)S(1)}, u32[]{:S(2)}, u32[]{:S(2)}) collective-permute-start(bf16[2,384,384]{2,1,0:T(8,128)(2,1)S(1)} %bitcast.60), channel_id=1, source_target_pairs={{0,128},{128,0},{1,129},{129,1},{2,130},{130,2},{3,131},{131,3},{4... | collective-permute-start | bytes 1769480 | tf_op jit(solution)/shard_map/ppermute | solution.py:256
  17.5 1.0 copy-start.10
  17.5 16.9 %copy-start.3 = (bf16[1,384,384]{2,1,0:T(8,128)(2,1)S(1)}, bf16[1,384,384]{2,1,0:T(8,128)(2,1)}, u32[]{:S(2)}) copy-start(bf16[1,384,384]{2,1,0:T(8,128)(2,1)} %param.12) | copy-start | bytes 884740
  17.5 17.6 %copy-start.4 = (bf16[1,384,384]{2,1,0:T(8,128)(2,1)S(1)}, bf16[1,384,384]{2,1,0:T(8,128)(2,1)}, u32[]{:S(2)}) copy-start(bf16[1,384,384]{2,1,0:T(8,128)(2,1)} %param.13) | copy-start | bytes 884740
  17.6 49.3 %copy-start = (bf16[2,2,384,384]{3,2,1,0:T(8,128)(2,1)}, bf16[2,2,384,384]{3,2,1,0:T(8,128)(2,1)S(1)}, u32[]{:S(2)}) copy-start(bf16[2,2,384,384]{3,2,1,0:T(8,128)(2,1)S(1)} %pad_maximum_fusion.w_near) | copy-start | bytes 3538948
  17.6 27.4 %copy-start.12 = (s32[8,1]{0,1:T(1,128)S(1)}, s32[8,1]{0,1:T(1,128)}, u32[]{:S(2)}) copy-start(s32[8,1]{0,1:T(1,128)} %param.20) | copy-start | bytes 100
  17.6 28.2 %copy-start.11 = (s32[1,2]{1,0:T(1,128)S(1)}, s32[1,2]{1,0:T(1,128)}, u32[]{:S(2)}) copy-start(s32[1,2]{1,0:T(1,128)} %param.19) | copy-start | bytes 28
  17.7 49.2 %collective-permute-start.11 = (bf16[2,2,384,384]{3,2,1,0:T(8,128)(2,1)S(1)}, bf16[2,2,384,384]{3,2,1,0:T(8,128)(2,1)S(1)}, u32[]{:S(2)}, u32[]{:S(2)}) collective-permute-start(bf16[2,2,384,384]{3,2,1,0:T(8,128)(2,1)S(1)} %pad_maximum_fusion.w_near), channel_id=1, source_target_pairs={{0,64},{64,0},{1,65},{65,1},{2,66},{66,2},{3,67},{67,3},{4,68},{68... | collective-permute-start | bytes 3538952 | tf_op jit(solution)/shard_map/ppermute | solution.py:258
  18.4 12.1 %collective-permute-start.5 = (bf16[384,384]{1,0:T(8,128)(2,1)S(1)}, bf16[384,384]{1,0:T(8,128)(2,1)}, u32[]{:S(2)}, u32[]{:S(2)}) collective-permute-start(bf16[384,384]{1,0:T(8,128)(2,1)S(1)} %bitcast.73), channel_id=1, source_target_pairs={{0,7},{1,0},{2,1},{3,2},{4,3},{5,4},{6,5},{7,6},{8,15},{9,8},{10,9... | collective-permute-start | bytes 884744 | tf_op jit(solution)/shard_map/ppermute | solution.py:246
  24.3 10.0 %collective-permute-start.2 = (bf16[384,384]{1,0:T(8,128)(2,1)S(1)}, bf16[384,384]{1,0:T(8,128)(2,1)}, u32[]{:S(2)}, u32[]{:S(2)}) collective-permute-start(bf16[384,384]{1,0:T(8,128)(2,1)S(1)} %bitcast.74), channel_id=1, source_target_pairs={{0,1},{1,2},{2,3},{3,4},{4,5},{5,6},{6,7},{7,0},{8,9},{9,10},{10,1... | collective-permute-start | bytes 884744 | tf_op jit(solution)/shard_map/ppermute | solution.py:245
  30.5 11.1 %collective-permute-start.6 = (bf16[384,384]{1,0:T(8,128)(2,1)}, bf16[384,384]{1,0:T(8,128)(2,1)}, u32[]{:S(2)}, u32[]{:S(2)}) collective-permute-start(bf16[384,384]{1,0:T(8,128)(2,1)} %collective-permute-done.5.s2), channel_id=1, source_target_pairs={{0,7},{1,0},{2,1},{3,2},{4,3},{5,4},{6,5},{7,6},{8,15},{9,8},{10,9... | collective-permute-start | bytes 884744 | tf_op jit(solution)/shard_map/ppermute | solution.py:246
  34.3 10.7 %collective-permute-start.3 = (bf16[384,384]{1,0:T(8,128)(2,1)}, bf16[384,384]{1,0:T(8,128)(2,1)}, u32[]{:S(2)}, u32[]{:S(2)}) collective-permute-start(bf16[384,384]{1,0:T(8,128)(2,1)} %collective-permute-done.2.s1), channel_id=1, source_target_pairs={{0,1},{1,2},{2,3},{3,4},{4,5},{5,6},{6,7},{7,0},{8,9},{9,10},{10,1... | collective-permute-start | bytes 884744 | tf_op jit(solution)/shard_map/ppermute | solution.py:245
  35.8 23.5 %collective-permute-start.1 = (bf16[2,384,384]{2,1,0:T(8,128)(2,1)}, bf16[2,384,384]{2,1,0:T(8,128)(2,1)S(1)}, u32[]{:S(2)}, u32[]{:S(2)}) collective-permute-start(bf16[2,384,384]{2,1,0:T(8,128)(2,1)} %constant_dynamic-update-slice_fusion), channel_id=1, source_target_pairs={{8,0},{16,8},{24,16},{32,24},{40,32},{48,40},{56,48},{9,1},{17,9},... | collective-permute-start | bytes 1769480 | tf_op jit(solution)/shard_map/ppermute | solution.py:253
  38.3 21.0 %collective-permute-start = (bf16[2,384,384]{2,1,0:T(8,128)(2,1)}, bf16[2,384,384]{2,1,0:T(8,128)(2,1)S(1)}, u32[]{:S(2)}, u32[]{:S(2)}) collective-permute-start(bf16[2,384,384]{2,1,0:T(8,128)(2,1)} %constant_dynamic-update-slice_fusion), channel_id=1, source_target_pairs={{0,8},{8,16},{16,24},{24,32},{32,40},{40,48},{48,56},{1,9},{9,17},... | collective-permute-start | bytes 1769480 | tf_op jit(solution)/shard_map/ppermute | solution.py:252
  41.7 7.9 %collective-permute-start.7 = (bf16[384,384]{1,0:T(8,128)(2,1)}, bf16[384,384]{1,0:T(8,128)(2,1)S(1)}, u32[]{:S(2)}, u32[]{:S(2)}) collective-permute-start(bf16[384,384]{1,0:T(8,128)(2,1)} %collective-permute-done.6.s4), channel_id=1, source_target_pairs={{0,7},{1,0},{2,1},{3,2},{4,3},{5,4},{6,5},{7,6},{8,15},{9,8},{10,9... | collective-permute-start | bytes 884744 | tf_op jit(solution)/shard_map/ppermute | solution.py:246
  45.0 9.6 %collective-permute-start.4 = (bf16[384,384]{1,0:T(8,128)(2,1)}, bf16[384,384]{1,0:T(8,128)(2,1)S(1)}, u32[]{:S(2)}, u32[]{:S(2)}) collective-permute-start(bf16[384,384]{1,0:T(8,128)(2,1)} %collective-permute-done.3.s3), channel_id=1, source_target_pairs={{0,1},{1,2},{2,3},{3,4},{4,5},{5,6},{6,7},{7,0},{8,9},{9,10},{10,1... | collective-permute-start | bytes 884744 | tf_op jit(solution)/shard_map/ppermute | solution.py:245
  49.6 0.7 copy-start.8
  51.0 22.6 %collective-permute-start.9 = (bf16[192,384]{1,0:T(8,128)(2,1)}, bf16[192,384]{1,0:T(8,128)(2,1)}, u32[]{:S(2)}, u32[]{:S(2)}) collective-permute-start(bf16[192,384]{1,0:T(8,128)(2,1)} %slice.59), channel_id=1, source_target_pairs={{0,7},{1,0},{2,1},{3,2},{4,3},{5,4},{6,5},{7,6},{8,15},{9,8},{10,9... | collective-permute-start | bytes 442376 | tf_op jit(solution)/shard_map/ppermute | solution.py:249
  54.6 0.7 copy-start.9
  56.0 17.6 %collective-permute-start.8 = (bf16[192,384]{1,0:T(8,128)(2,1)}, bf16[192,384]{1,0:T(8,128)(2,1)}, u32[]{:S(2)}, u32[]{:S(2)}) collective-permute-start(bf16[192,384]{1,0:T(8,128)(2,1)} %slice.58), channel_id=1, source_target_pairs={{0,1},{1,2},{2,3},{3,4},{4,5},{5,6},{6,7},{7,0},{8,9},{9,10},{10,1... | collective-permute-start | bytes 442376 | tf_op jit(solution)/shard_map/ppermute | solution.py:248
  59.3 0.9 copy-start.5
  59.3 1.1 copy-start.6
  66.9 1.0 copy-start.2
  81.8 18.1 %collective-permute-start.14 = (bf16[2,2,384,384]{3,2,1,0:T(8,128)(2,1)}, bf16[2,2,384,384]{3,2,1,0:T(8,128)(2,1)}, u32[]{:S(2)}, u32[]{:S(2)}) collective-permute-start(bf16[2,2,384,384]{3,2,1,0:T(8,128)(2,1)} %slice_bitcast_fusion), channel_id=1, source_target_pairs={{0,64},{64,0},{1,65},{65,1},{2,66},{66,2},{3,67},{67,3},{4,68},{68... | collective-permute-start | bytes 3538952 | tf_op jit(solution)/shard_map/ppermute | solution.py:270
  81.8 18.1 %copy-start.1 = (bf16[2,2,2,384,384]{4,3,2,1,0:T(8,128)(2,1)S(1)}, bf16[2,2,2,384,384]{4,3,2,1,0:T(8,128)(2,1)}, u32[]{:S(2)}) copy-start(bf16[2,2,2,384,384]{4,3,2,1,0:T(8,128)(2,1)} %get-tuple-element.26) | copy-start | bytes 7077892
  91.7 17.9 %all-to-all-start.1 = ((bf16[8,2,32,384]{3,2,1,0:T(8,128)(2,1)}), bf16[8,2,32,384]{3,2,1,0:T(8,128)(2,1)S(1)}, u32[]{:S(2)}, u32[]{:S(2)}) async-start(bf16[8,2,32,384]{3,2,1,0:T(8,128)(2,1)} %bitcast.50), calls=%async_computation.1 | async-start | bytes 786432 | tf_op jit(solution)/shard_map/all_to_all | solution.py:282
  109.6 23.3 %all-to-all-start = ((bf16[16,2,48,384]{3,2,1,0:T(8,128)(2,1)}), bf16[16,2,48,384]{3,2,1,0:T(8,128)(2,1)S(1)}, u32[]{:S(2)}, u32[]{:S(2)}) async-start(bf16[16,2,48,384]{3,2,1,0:T(8,128)(2,1)} %bitcast.22), calls=%async_computation | async-start | bytes 2359296 | tf_op jit(solution)/shard_map/all_to_all | solution.py:275
  114.3 27.9 %collective-permute-start.12 = (bf16[2,384,384]{2,1,0:T(8,128)(2,1)}, bf16[2,384,384]{2,1,0:T(8,128)(2,1)S(1)}, u32[]{:S(2)}, u32[]{:S(2)}) collective-permute-start(bf16[2,384,384]{2,1,0:T(8,128)(2,1)} %get-tuple-element.24), channel_id=1, source_target_pairs={{8,0},{16,8},{24,16},{32,24},{40,32},{48,40},{56,48},{9,1},{17,9},... | collective-permute-start | bytes 1769480 | tf_op jit(solution)/shard_map/ppermute | solution.py:285
  116.4 29.7 %collective-permute-start.13 = (bf16[2,384,384]{2,1,0:T(8,128)(2,1)}, bf16[2,384,384]{2,1,0:T(8,128)(2,1)}, u32[]{:S(2)}, u32[]{:S(2)}) collective-permute-start(bf16[2,384,384]{2,1,0:T(8,128)(2,1)} %get-tuple-element.25), channel_id=1, source_target_pairs={{0,8},{8,16},{16,24},{24,32},{32,40},{40,48},{48,56},{1,9},{9,17},... | collective-permute-start | bytes 1769480 | tf_op jit(solution)/shard_map/ppermute | solution.py:286
  134.2 11.9 %copy-start.7 = (f32[2,384,384]{2,1,0:T(8,128)S(1)}, f32[2,384,384]{2,1,0:T(8,128)}, u32[]{:S(2)}) copy-start(f32[2,384,384]{2,1,0:T(8,128)} %get-tuple-element.23) | copy-start | bytes 3538948
  134.2 21.0 %all-to-all-start.2 = ((bf16[8,160,384]{2,1,0:T(8,128)(2,1)}), bf16[8,160,384]{2,1,0:T(8,128)(2,1)S(1)}, u32[]{:S(2)}, u32[]{:S(2)}) async-start(bf16[8,160,384]{2,1,0:T(8,128)(2,1)} %broadcast_in_dim.18), calls=%async_computation.2 | async-start | bytes 1966080 | tf_op jit(solution)/shard_map/all_to_all | solution.py:293

commit v2 on v1

v2 whole, which is shorter than its diff:
```python
import jax
import jax.numpy as jnp
from jax import lax
from jax.experimental import pallas as pl
from jax.experimental.pallas import tpu as pltpu
from jax.sharding import Mesh, PartitionSpec as P


HD = 128
B16 = jnp.bfloat16
F32 = jnp.float32
NEG = -1e30
LOG2E = 1.4426950408889634

VM = pltpu.MemorySpace.VMEM
SM = pltpu.MemorySpace.SMEM


def vspec():
    return pl.BlockSpec(memory_space=VM)


def sspec():
    return pl.BlockSpec(memory_space=SM)


def nn(a, b):
    return lax.dot_general(a, b, (((1,), (0,)), ((), ())), preferred_element_type=F32)


def nt(a, b):
    return lax.dot_general(a, b, (((1,), (1,)), ((), ())), preferred_element_type=F32)


def in_hbm(*arrays):
    return tuple(pltpu.with_memory_space_constraint(array, pltpu.HBM) for array in arrays)


def call(kernel, outs, args, scalars=0, hbm_outs=()):
    return pl.pallas_call(
        kernel,
        out_shape=tuple(
            pltpu.HBM(shape, dtype) if place in hbm_outs else jax.ShapeDtypeStruct(shape, dtype)
            for place, (shape, dtype) in enumerate(outs)
        ),
        in_specs=[sspec()] * scalars + [vspec()] * (len(args) - scalars),
        out_specs=(vspec(),) * len(outs),
        compiler_params=pltpu.CompilerParams(vmem_limit_bytes=16 << 20),
    )(*args)


def ring(count, step):
    return [(i, (i + step) % count) for i in range(count)]


def forward_kernel(windows, tile_map, count, q, kown, vown, prev, nxt, tk, tv, probs, text_probs, att_t):
    tok, width = q.shape
    txt = tk.shape[0]
    slabs = tile_map.shape[0]
    index = lax.axis_index("sp")
    visible = []
    for step in (-1, 0, 1):
        other = index + step
        apart = tile_map[index] - tile_map[jnp.clip(other, 0, slabs - 1)]
        visible.append(
            (abs(step) <= windows[0])
            & (jnp.abs(apart) <= windows[1])
            & (other >= 0)
            & (other < slabs)
        )
    factor = HD ** (-0.5) * LOG2E
    for h in range(width // HD):
        cols = slice(h * HD, (h + 1) * HD)
        qh = q[:, cols]
        keys = [prev[0, :, cols], kown[:, cols], nxt[0, :, cols]]
        scores = [jnp.where(visible[place], nt(keys[place], qh), NEG) for place in range(3)]
        live = lax.broadcasted_iota(jnp.int32, (txt, tok), 0) < count[0]
        scores.append(jnp.where(live, nt(tk[:, cols], qh), NEG))
        top = scores[0].max(axis=0, keepdims=True)
        for s in scores[1:]:
            top = jnp.maximum(top, s.max(axis=0, keepdims=True))
        shift = top * factor
        total = jnp.zeros((1, tok), F32)
        expd = []
        for s in scores:
            e = jnp.exp2(s * factor - shift)
            total = total + e.sum(axis=0, keepdims=True)
            expd.append(e)
        inverse = 1.0 / total
        values = [prev[1, :, cols], vown[:, cols], nxt[1, :, cols], tv[:, cols]]
        out = jnp.zeros((HD, tok), F32)
        for place, (e, v) in enumerate(zip(expd, values)):
            p = (e * inverse).astype(B16)
            if place < 3:
                probs[h, place] = p
            else:
                text_probs[h] = p
            out = out + nn(v.T, p)
        att_t[cols, :] = out.astype(B16)


def block_weight(block, dp, pieces):
    size = pieces[0].shape[1] // 2
    side = pl.multiple_of((block & 1) * size, 128)
    diff = (block >> 1) ^ dp
    near, far, up, down, far_up, far_down = [piece[:, pl.ds(side, size)] for piece in pieces]
    same = (diff & 1) == 0
    low = jnp.where(same, near, far)
    high = jnp.concatenate([jnp.where(same, up, far_up), jnp.where(same, down, far_down)], axis=0)
    return jnp.where(diff < 2, low, high)


def contract_shard(block, shard, gate, pieces, att_t):
    dp = lax.axis_index("dy") * 2 + lax.axis_index("dc")
    scaled = (shard.astype(F32) * gate[block].astype(F32)).astype(B16)
    part = nn(att_t, scaled).astype(B16)
    return nt(block_weight(block, dp, pieces), scaled), part


EARLY = (0, 7, 1, 6, 2)
LATE = (5, 3, 4)


def early_kernel(s0, s1, s2, s3, s4, gate, w0, w1, w2a, w2b, w3a, w3b, att, acc, parts):
    t = lax.axis_index("tp")
    att_t = att[...]
    total = None
    for place, ref in enumerate((s0, s1, s2, s3, s4)):
        grad, part = contract_shard(
            (t + EARLY[place]) & 7, ref[...], gate, (w0, w1, w2a, w2b, w3a, w3b), att_t
        )
        parts[place] = part
        total = grad if total is None else total + grad
    acc[...] = total


def late_kernel(s5, s6, s7a, s7b, gate, w0, w1, w2a, w2b, w3a, w3b, att, acc, parts, ga, keep, send):
    t = lax.axis_index("tp")
    core = lax.axis_index("dc")
    att_t = att[...]
    count, cut = keep.shape[0], keep.shape[3]

    def put(block, part):
        owner = block >> 1
        cells = part.reshape(count, cut, part.shape[1])

        @pl.when((owner & 1) == core)
        def _():
            keep[:, block & 1, owner >> 1] = cells

        @pl.when((owner & 1) != core)
        def _():
            send[:, block & 1, owner >> 1] = cells

    total = acc[...]
    shards = (s5[...], s6[...], jnp.concatenate([s7a[...], s7b[...]], axis=0))
    for step, shard in zip(LATE, shards):
        block = (t + step) & 7
        grad, part = contract_shard(block, shard, gate, (w0, w1, w2a, w2b, w3a, w3b), att_t)
        put(block, part)
        total = total + grad
    for place, step in enumerate(EARLY):
        put((t + step) & 7, parts[place])
    ga[...] = total.astype(B16)


def head_terms(h, q, att, gat):
    cols = slice(h * HD, (h + 1) * HD)
    ga_t = gat[cols, :]
    delta = jnp.sum(ga_t.astype(F32) * att[cols, :].astype(F32), axis=0, keepdims=True)
    return cols, q[:, cols], ga_t, ga_t.T, delta


def piece_grads(p_t, key, value, qh, ga_t, ga, delta):
    grad_p = nn(value, ga_t)
    ds_t = (p_t.astype(F32) * (grad_p - delta)).astype(B16)
    factor = HD ** (-0.5)
    return nn(key.T, ds_t), factor * nn(ds_t, qh), nn(p_t, ga)


def text_kernel(q, tk, tv, probs, att, gat, gtext, gq_t):
    _, width = q.shape
    count, tcut = gtext.shape[0], gtext.shape[1] // 2
    for h in range(width // HD):
        cols, qh, ga_t, ga, delta = head_terms(h, q, att, gat)
        p_t = probs[h]
        dq, gk, gv = piece_grads(p_t, tk[:, cols], tv[:, cols], qh, ga_t, ga, delta)
        gtext[:, :tcut, cols] = gk.astype(B16).reshape(count, tcut, HD)
        gtext[:, tcut:, cols] = gv.astype(B16).reshape(count, tcut, HD)
        gq_t[cols, :] = dq


def video_kernel(q, kown, vown, prev, nxt, probs, att, gat, gq_in, gq, gprev, gown, gnext):
    _, width = q.shape
    factor = HD ** (-0.5)
    for h in range(width // HD):
        cols, qh, ga_t, ga, delta = head_terms(h, q, att, gat)
        gq_t = gq_in[cols, :]
        pieces = (
            (0, prev[0, :, cols], prev[1, :, cols], gprev),
            (2, nxt[0, :, cols], nxt[1, :, cols], gnext),
            (1, kown[:, cols], vown[:, cols], gown),
        )
        for place, key, value, out in pieces:
            p_t = probs[h, place]
            dq, gk, gv = piece_grads(p_t, key, value, qh, ga_t, ga, delta)
            out[0, :, cols] = gk.astype(out.dtype)
            out[1, :, cols] = gv.astype(out.dtype)
            gq_t = gq_t + dq
        gq[:, cols] = (factor * gq_t).T.astype(B16)


def pack_kernel(keep, other, gtext, out):
    rows = keep.shape[1]
    out[:, :rows] = (keep[...].astype(F32) + other[...].astype(F32)).astype(B16)
    out[:, rows:] = gtext[...]


def halo_kernel(own, later, earlier, gk, gv):
    for place, out in enumerate((gk, gv)):
        total = own[place] + later[place].astype(F32) + earlier[place].astype(F32)
        out[...] = total.astype(B16)


def merge_kernel(cells, out):
    count = cells.shape[0]
    cut = cells.shape[1] - out.shape[1]
    span = count // 2
    words = []
    for side in range(2):
        total = cells[side * span, 2 * cut :].astype(F32)
        for place in range(1, span):
            total = total + cells[side * span + place, 2 * cut :].astype(F32)
        words.append(total.astype(B16))
    total = cells[0, : 2 * cut].astype(F32)
    for place in range(1, count):
        total = total + cells[place, : 2 * cut].astype(F32)
    total = total.astype(B16)
    for place in range(count):
        side = place // span
        out[place, :cut] = total[side * cut : (side + 1) * cut]
        out[place, cut:] = words[side]


def unpack_kernel(cells, weight, text_k, text_v):
    count, _, width = cells.shape
    cut = 2 * weight.shape[0] // count
    tcut = text_k.shape[0] // count
    for place in range(count):
        row, col = (place // 2) * cut, (place % 2) * width
        weight[row : row + cut, col : col + width] = cells[place, :cut].astype(F32)
        text_k[place * tcut : (place + 1) * tcut] = cells[place, cut : cut + tcut]
        text_v[place * tcut : (place + 1) * tcut] = cells[place, cut + tcut :]


def y_routes(sp):
    count = sp // 2

    def place(y, x):
        return (y % 2) * sp + (y // 2) * count + x

    spots = [(y, x) for y in range(4) for x in range(count)]
    up = [(place(y, x), place((y + 1) % 4, x)) for y, x in spots]
    down = [(place(y, x), place((y - 1) % 4, x)) for y, x in spots]
    return up, down


def device_program(
    query, key, value, text_key, text_value, grad_out, gate, out_weight, windows, tile_map, text_count
):
    sp = lax.axis_size("sp")
    tp = lax.axis_size("tp")
    tok, width = query.shape[1], query.shape[2]
    txt = text_key.shape[1]
    rows = out_weight.shape[0]
    wide = grad_out.shape[2]
    count = 2 * sp
    cut, tcut = rows // sp, txt // count
    later = [(i, i + 1) for i in range(sp - 1)]
    earlier = [(i + 1, i) for i in range(sp - 1)]
    swap = [(0, 1), (1, 0)]

    own = grad_out[0]
    right = [own]
    left = [own]
    for _ in range(3):
        right.append(lax.ppermute(right[-1], "tp", ring(tp, 1)))
        left.append(lax.ppermute(left[-1], "tp", ring(tp, -1)))
    half = tok // 2
    last_a = lax.ppermute(right[3][:half], "tp", ring(tp, 1))
    last_b = lax.ppermute(left[3][half:], "tp", ring(tp, -1))

    pair = jnp.stack([key[0], value[0]], axis=0)
    prev = lax.ppermute(pair, "sp", later)
    nxt = lax.ppermute(pair, "sp", earlier)

    w0 = out_weight
    w1 = lax.ppermute(w0, "dc", swap)
    up, down = y_routes(sp)
    mid = rows // 2
    w2a = lax.ppermute(w0[:mid], ("dy", "sp"), up)
    w2b = lax.ppermute(w0[mid:], ("dy", "sp"), down)
    w3a = lax.ppermute(w2a, "dc", swap)
    w3b = lax.ppermute(w2b, "dc", swap)
    gates = gate[0].reshape(tp, 1, -1)

    q, k, v, tk, tv = in_hbm(query[0], key[0], value[0], text_key[0], text_value[0])
    (own_hbm, gates, w0) = in_hbm(own, gates, w0)
    probs, text_probs, att_t = call(
        forward_kernel,
        [
            ((width // HD, 3, tok, tok), B16),
            ((width // HD, txt, tok), B16),
            ((width, tok), B16),
        ],
        (windows[0], tile_map.reshape(-1), text_count, q, k, v, prev, nxt, tk, tv),
        scalars=3,
        hbm_outs=(0,),
    )
    acc, parts = call(
        early_kernel,
        [((width, tok), F32), ((len(EARLY), width, own.shape[1]), B16)],
        (own_hbm, right[1], left[1], right[2], left[2], gates, w0, w1, w2a, w2b, w3a, w3b, att_t),
    )
    cells = (count // 2, 2, 2, cut, wide)
    ga_t, keep, send = call(
        late_kernel,
        [((width, tok), B16), (cells, B16), (cells, B16)],
        (right[3], left[3], last_a, last_b, gates, w0, w1, w2a, w2b, w3a, w3b, att_t, acc, parts),
    )

    other = lax.ppermute(send, "dc", swap)
    gtext, gq_t = call(
        text_kernel,
        [((count, 2 * tcut, width), B16), ((width, tok), F32)],
        (q, tk, tv, text_probs, att_t, ga_t),
        hbm_outs=(1,),
    )
    (packed,) = call(
        pack_kernel,
        [((count, 2 * cut + 2 * tcut, wide), B16)],
        (keep.reshape(count, 2 * cut, wide), other.reshape(count, 2 * cut, wide), gtext),
    )
    arrived = lax.all_to_all(packed, ("dy", "sp"), 0, 0, tiled=True)

    gq, gprev, gown, gnext = call(
        video_kernel,
        [
            ((tok, width), B16),
            ((2, tok, width), B16),
            ((2, tok, width), F32),
            ((2, tok, width), B16),
        ],
        (q, k, v, *in_hbm(prev, nxt, probs, att_t, ga_t, gq_t)),
    )
    from_later = lax.ppermute(gprev, "sp", earlier)
    from_earlier = lax.ppermute(gnext, "sp", later)
    total_k, total_v = call(
        halo_kernel, [((tok, width), B16)] * 2, (gown, from_later, from_earlier)
    )

    (copies,) = call(merge_kernel, [((count, cut + 2 * tcut, wide), B16)], (arrived,))
    gathered = lax.all_to_all(copies, ("dy", "sp"), 0, 0, tiled=True)
    weight, text_k, text_v = call(
        unpack_kernel,
        [((rows, 2 * wide), F32), ((txt, width), B16), ((txt, width), B16)],
        (gathered,),
    )
    return (gq[None], total_k[None], total_v[None], text_k[None], text_v[None], weight)


def solution(mesh):
    shape = mesh.devices.shape
    fine = Mesh(mesh.devices.reshape(2, shape[0] // 2, *shape[1:]), ("dy", "dc", "sp", "tp"))
    dp = ("dy", "dc")
    placed = (
        P(dp, "sp", "tp"),
        P(dp, "sp", "tp"),
        P(dp, "sp", "tp"),
        P(dp, None, "tp"),
        P(dp, None, "tp"),
        P(dp, "sp", "tp"),
        P(dp, None),
        P("tp", dp),
        P("sp", None),
        P(),
        P(dp),
    )
    return jax.shard_map(
        device_program,
        mesh=fine,
        in_specs=placed,
        out_specs=(
            P(dp, "sp", "tp"),
            P(dp, "sp", "tp"),
            P(dp, "sp", "tp"),
            P(dp, None, "tp"),
            P(dp, None, "tp"),
            P("tp", dp),
        ),
        check_vma=False,
    )
```

time: 159 us -> 125 us (0.79)
  the two profiles are of different devices: /device:TPU:2 before, /device:TPU:24 now
where the time goes in v2:
time: 125 us; the launch traced here: 124 us
  starting transfers between devices  37.3 us (30%)
  waiting for transfers between devices  32.1 us (26%)
  Pallas kernels  26.1 us (21%)
  blocking collectives  26.1 us (21%)
  between operations  1.58 us (1%)
  local copies, waits for them, and re-layouts  1.25 us (1%)
    all_to_all x1, blocking collectives, device_program(): arrived = lax.all_to_all(packed, ('dy', 'sp'), 0, 0, tiled=True)  26.1 us
    pallas_call x9, Pallas kernels, call(): pl.pallas_call(kernel, out_shape=tuple((pltpu.HBM(shape, dtype) if place...  26.1 us
    ppermute x3, starting transfers between devices, device_program(): left.append(lax.ppermute(left[-1], 'tp', ring(tp, -1)))  12.8 us
    ppermute x1, waiting for transfers between devices, device_program(): from_later = lax.ppermute(gprev, 'sp', earlier)  10.1 us
    ppermute x1, waiting for transfers between devices, device_program(): from_earlier = lax.ppermute(gnext, 'sp', later)  7.19 us
    ppermute x3, waiting for transfers between devices, device_program(): left.append(lax.ppermute(left[-1], 'tp', ring(tp, -1)))  6.6 us
    ppermute x1, starting transfers between devices, device_program(): from_later = lax.ppermute(gprev, 'sp', earlier)  5.46 us
    ppermute x1, starting transfers between devices, device_program(): nxt = lax.ppermute(pair, 'sp', earlier)  5.34 us
  transfers between devices with their start and end apart: 19, of which 6 were waited for; matrix products, arithmetic and copies ran while one was open for 1% of the time, Pallas kernels for 16%

profile of v2, /device:TPU:24, one launch (start us, length us, event | category | flops | bytes accessed | tf_op | source)
XLA Modules:
  0.0 124.5 jit_solution(1411134897269228425)
XLA Ops:
  0.6 0.0 copy-start.7
  0.6 0.0 copy-start.8
  0.7 5.9 %collective-permute-start.5 = (bf16[384,384]{1,0:T(8,128)(2,1)}, bf16[384,384]{1,0:T(8,128)(2,1)S(1)}, u32[]{:S(2)}, u32[]{:S(2)}) collective-permute-start(bf16[384,384]{1,0:T(8,128)(2,1)} %bitcast.31), channel_id=1, source_target_pairs={{0,7},{1,0},{2,1},{3,2},{4,3},{5,4},{6,5},{7,6},{8,15},{9,8},{10,9... | collective-permute-start | bytes 884744 | tf_op jit(solution)/shard_map/ppermute | solution.py:288
  6.6 1.1 fusion
  7.7 0.8 collective-permute-start.12
  8.5 2.5 %collective-permute-start.11 = (bf16[192,768]{1,0:T(8,128)(2,1)S(1)}, bf16[192,768]{1,0:T(8,128)(2,1)S(1)}, u32[]{:S(2)}, u32[]{:S(2)}) collective-permute-start(bf16[192,768]{1,0:T(8,128)(2,1)S(1)} %get-tuple-element.45), channel_id=1, source_target_pairs={{0,128},{8,136},{16,144},{24,152},{128,32},{136,40},{144,48},{152,... | collective-permute-start | bytes 884744 | tf_op jit(solution)/shard_map/ppermute | solution.py:301
  11.0 2.1 %collective-permute-done.5.s2 = bf16[384,384]{1,0:T(8,128)(2,1)S(1)} collective-permute-done((bf16[384,384]{1,0:T(8,128)(2,1)}, bf16[384,384]{1,0:T(8,128)(2,1)S(1)}, u32[]{:S(2)}, u32[]{:S(2)}) %collective-permute-start.5) | collective-permute-done | bytes 294944 | tf_op jit(solution)/shard_map/ppermute | solution.py:288
  13.2 3.6 %collective-permute-start.6 = (bf16[384,384]{1,0:T(8,128)(2,1)S(1)}, bf16[384,384]{1,0:T(8,128)(2,1)S(1)}, u32[]{:S(2)}, u32[]{:S(2)}) collective-permute-start(bf16[384,384]{1,0:T(8,128)(2,1)S(1)} %collective-permute-done.5.s2), channel_id=1, source_target_pairs={{0,7},{1,0},{2,1},{3,2},{4,3},{5,4},{6,5},{7,6},{8,15},{9,8},{10,9... | collective-permute-start | bytes 884744 | tf_op jit(solution)/shard_map/ppermute | solution.py:288
  16.9 5.3 %collective-permute-start.1 = (bf16[2,384,384]{2,1,0:T(8,128)(2,1)S(1)}, bf16[2,384,384]{2,1,0:T(8,128)(2,1)S(1)}, u32[]{:S(2)}, u32[]{:S(2)}) collective-permute-start(bf16[2,384,384]{2,1,0:T(8,128)(2,1)S(1)} %constant_dynamic-update-slice_fusion), channel_id=1, source_target_pairs={{8,0},{16,8},{24,16},{32,24},{40,32},{48,40},{56,48},{9,1},{17,9},... | collective-permute-start | bytes 1769480 | tf_op jit(solution)/shard_map/ppermute | solution.py:295
  22.2 1.9 %collective-permute-start = (bf16[2,384,384]{2,1,0:T(8,128)(2,1)S(1)}, bf16[2,384,384]{2,1,0:T(8,128)(2,1)S(1)}, u32[]{:S(2)}, u32[]{:S(2)}) collective-permute-start(bf16[2,384,384]{2,1,0:T(8,128)(2,1)S(1)} %constant_dynamic-update-slice_fusion), channel_id=1, source_target_pairs={{0,8},{8,16},{16,24},{24,32},{32,40},{40,48},{48,56},{1,9},{9,17},... | collective-permute-start | bytes 1769480 | tf_op jit(solution)/shard_map/ppermute | solution.py:294
  24.2 3.3 %collective-permute-start.7 = (bf16[384,384]{1,0:T(8,128)(2,1)S(1)}, bf16[384,384]{1,0:T(8,128)(2,1)S(1)}, u32[]{:S(2)}, u32[]{:S(2)}) collective-permute-start(bf16[384,384]{1,0:T(8,128)(2,1)S(1)} %collective-permute-done.6.s4), channel_id=1, source_target_pairs={{0,7},{1,0},{2,1},{3,2},{4,3},{5,4},{6,5},{7,6},{8,15},{9,8},{10,9... | collective-permute-start | bytes 884744 | tf_op jit(solution)/shard_map/ppermute | solution.py:288
  27.5 0.1 collective-permute-start.10
  27.6 4.4 %collective-permute-done.7.s6 = bf16[384,384]{1,0:T(8,128)(2,1)S(1)} collective-permute-done((bf16[384,384]{1,0:T(8,128)(2,1)S(1)}, bf16[384,384]{1,0:T(8,128)(2,1)S(1)}, u32[]{:S(2)}, u32[]{:S(2)}) %collective-permute-start.7) | collective-permute-done | bytes 294944 | tf_op jit(solution)/shard_map/ppermute | solution.py:288
  32.1 3.4 %collective-permute-done.4.s5 = bf16[384,384]{1,0:T(8,128)(2,1)S(1)} collective-permute-done((bf16[384,384]{1,0:T(8,128)(2,1)S(1)}, bf16[384,384]{1,0:T(8,128)(2,1)S(1)}, u32[]{:S(2)}, u32[]{:S(2)}) %collective-permute-start.4) | collective-permute-done | bytes 294944 | tf_op jit(solution)/shard_map/ppermute | solution.py:287
  35.5 1.1 collective-permute-start.9
  36.6 4.8 %collective-permute-done.prev = bf16[2,384,384]{2,1,0:T(8,128)(2,1)S(1)} collective-permute-done((bf16[2,384,384]{2,1,0:T(8,128)(2,1)S(1)}, bf16[2,384,384]{2,1,0:T(8,128)(2,1)S(1)}, u32[]{:S(2)}, u32[]{:S(2)}) %collective-permute-start) | collective-permute-done | bytes 589856 | tf_op jit(solution)/shard_map/ppermute | solution.py:294
  42.1 5.9 %shard_map.154 = (bf16[3,3,384,384]{3,2,1,0:T(8,128)(2,1)}, bf16[3,256,384]{2,1,0:T(8,128)(2,1)S(1)}, bf16[384,384]{1,0:T(8,128)(2,1)S(1)}) custom-call(s32[2]{0:T(128)S(1)} %bitcast.18, s32[8]{0:T(128)S(1)} %bitcast.19, s32[1]{0:T(128)S(6)} %copy.18.count, bf16[384,384]{1,0:T(8,128)(2,1)} %bitcast.20, bf16[384,384]{1,0:T(8,128)(2,1)} %bitcast.23, ...), custom_call_target="tpu_custom_call" | custom-call | tf_op jit(solution)/shard_map/pallas_call | solution.py:40
  48.0 3.3 %shard_map.155 = (f32[384,384]{1,0:T(8,128)S(1)}, bf16[5,384,384]{2,1,0:T(8,128)(2,1)S(1)}) custom-call(bf16[384,384]{1,0:T(8,128)(2,1)} %bitcast.33, bf16[384,384]{1,0:T(8,128)(2,1)S(1)} %collective-permute-done.2.s1, bf16[384,384]{1,0:T(8,128)(2,1)S(1)} %collective-permute-done.5.s2, bf16[384,384]{1,0:T(8,128)(2,1)S(1)} %collective-permute-done.3.s3, ...), custom_call_target="tpu_custom_call" | custom-call | tf_op jit(solution)/shard_map/pallas_call | solution.py:40
  51.4 3.3 %shard_map.156 = (bf16[384,384]{1,0:T(8,128)(2,1)S(1)}, bf16[8,2,2,48,384]{4,3,2,1,0:T(8,128)(2,1)S(1)}, bf16[8,2,2,48,384]{4,3,2,1,0:T(8,128)(2,1)S(1)}) custom-call(bf16[384,384]{1,0:T(8,128)(2,1)S(1)} %collective-permute-done.4.s5, bf16[384,384]{1,0:T(8,128)(2,1)S(1)} %collective-permute-done.7.s6, bf16[192,384]{1,0:T(8,128)(2,1)S(1)} %collective-permute-done.8.s7a, ...), custom_call_target="tpu_custom_call" | custom-call | tf_op jit(solution)/shard_map/pallas_call | solution.py:40
  54.6 0.1 collective-permute-start.17
  54.7 3.0 %shard_map.157 = (bf16[16,32,384]{2,1,0:T(8,128)(2,1)S(1)}, f32[384,384]{1,0:T(8,128)}) custom-call(bf16[384,384]{1,0:T(8,128)(2,1)} %bitcast.21, bf16[256,384]{1,0:T(8,128)(2,1)} %bitcast.28, bf16[256,384]{1,0:T(8,128)(2,1)} %bitcast.30, bf16[3,256,384]{2,1,0:T(8,128)(2,1)S(1)} %get-tuple-element.30.probs, bf16[384,384]{1,0:T(8,128)(2,1)S(1)} %get-tuple-element.26.att, ...), custom_call_target="tpu_custom_call" | custom-call | tf_op jit(solution)/shard_map/pallas_call | solution.py:40
  57.7 0.3 shard_map.160
  58.0 26.1 %all_to_all.10.cells = bf16[16,128,384]{2,1,0:T(8,128)(2,1)S(1)} all-to-all(bf16[16,128,384]{2,1,0:T(8,128)(2,1)S(1)} %shard_map.160), channel_id=1, replica_groups=mesh['dy'=2,'dc'=2,'sp'=8,'tp'=8] {'dy','sp'}, dimensions={0} | all-to-all | bytes 3145728 | tf_op jit(solution)/shard_map/all_to_all | solution.py:344
  84.2 1.2 shard_map.161
  85.3 5.3 %all-to-all-start.1 = ((bf16[16,80,384]{2,1,0:T(8,128)(2,1)}), bf16[16,80,384]{2,1,0:T(8,128)(2,1)S(1)}, u32[]{:S(2)}, u32[]{:S(2)}) async-start(bf16[16,80,384]{2,1,0:T(8,128)(2,1)} %shard_map.161), calls=%async_computation.1 | async-start | bytes 1966080 | tf_op jit(solution)/shard_map/all_to_all | solution.py:363
  90.6 7.0 %shard_map.158 = (bf16[384,384]{1,0:T(8,128)(2,1)}, bf16[2,384,384]{2,1,0:T(8,128)(2,1)S(1)}, f32[2,384,384]{2,1,0:T(8,128)S(1)}, bf16[2,384,384]{2,1,0:T(8,128)(2,1)S(1)}) custom-call(bf16[384,384]{1,0:T(8,128)(2,1)} %bitcast.22, bf16[384,384]{1,0:T(8,128)(2,1)} %bitcast.24, bf16[384,384]{1,0:T(8,128)(2,1)} %bitcast.26, bf16[2,384,384]{2,1,0:T(8,128)(2,1)} %copy-done.2, ...), custom_call_target="tpu_custom_call" | custom-call | tf_op jit(solution)/shard_map/pallas_call | solution.py:40
  97.6 5.5 %collective-permute-start.15 = (bf16[2,384,384]{2,1,0:T(8,128)(2,1)S(1)}, bf16[2,384,384]{2,1,0:T(8,128)(2,1)S(1)}, u32[]{:S(2)}, u32[]{:S(2)}) collective-permute-start(bf16[2,384,384]{2,1,0:T(8,128)(2,1)S(1)} %get-tuple-element.34), channel_id=1, source_target_pairs={{8,0},{16,8},{24,16},{32,24},{40,32},{48,40},{56,48},{9,1},{17,9},... | collective-permute-start | bytes 1769480 | tf_op jit(solution)/shard_map/ppermute | solution.py:356
  103.1 1.9 %collective-permute-start.16 = (bf16[2,384,384]{2,1,0:T(8,128)(2,1)S(1)}, bf16[2,384,384]{2,1,0:T(8,128)(2,1)S(1)}, u32[]{:S(2)}, u32[]{:S(2)}) collective-permute-start(bf16[2,384,384]{2,1,0:T(8,128)(2,1)S(1)} %get-tuple-element.35), channel_id=1, source_target_pairs={{0,8},{8,16},{16,24},{24,32},{32,40},{40,48},{48,56},{1,9},{9,17},... | collective-permute-start | bytes 1769480 | tf_op jit(solution)/shard_map/ppermute | solution.py:357
  105.0 10.1 %collective-permute-done.15.later = bf16[2,384,384]{2,1,0:T(8,128)(2,1)S(1)} collective-permute-done((bf16[2,384,384]{2,1,0:T(8,128)(2,1)S(1)}, bf16[2,384,384]{2,1,0:T(8,128)(2,1)S(1)}, u32[]{:S(2)}, u32[]{:S(2)}) %collective-permute-start.15) | collective-permute-done | bytes 589856 | tf_op jit(solution)/shard_map/ppermute | solution.py:356
  115.1 7.2 %collective-permute-done.16.earlier = bf16[2,384,384]{2,1,0:T(8,128)(2,1)S(1)} collective-permute-done((bf16[2,384,384]{2,1,0:T(8,128)(2,1)S(1)}, bf16[2,384,384]{2,1,0:T(8,128)(2,1)S(1)}, u32[]{:S(2)}, u32[]{:S(2)}) %collective-permute-start.16) | collective-permute-done | bytes 589856 | tf_op jit(solution)/shard_map/ppermute | solution.py:357
  122.3 0.9 shard_map.159
  123.2 1.2 %shard_map.162 = (f32[384,768]{1,0:T(8,128)}, bf16[256,384]{1,0:T(8,128)(2,1)}, bf16[256,384]{1,0:T(8,128)(2,1)}) custom-call(bf16[16,80,384]{2,1,0:T(8,128)(2,1)S(1)} %all-to-all-done.1.cells), custom_call_target="tpu_custom_call" | custom-call | tf_op jit(solution)/shard_map/pallas_call | solution.py:40
  (39 shorter events, 0.2 us)
Async XLA Ops:
  0.6 16.1 %copy-start.7 = (bf16[1,384,384]{2,1,0:T(8,128)(2,1)S(1)}, bf16[1,384,384]{2,1,0:T(8,128)(2,1)}, u32[]{:S(2)}) copy-start(bf16[1,384,384]{2,1,0:T(8,128)(2,1)} %param.12) | copy-start | bytes 884740
  0.6 16.2 %copy-start.8 = (bf16[1,384,384]{2,1,0:T(8,128)(2,1)S(1)}, bf16[1,384,384]{2,1,0:T(8,128)(2,1)}, u32[]{:S(2)}) copy-start(bf16[1,384,384]{2,1,0:T(8,128)(2,1)} %param.13) | copy-start | bytes 884740
  0.7 26.8 %copy-start.6 = (bf16[384,768]{1,0:T(8,128)(2,1)S(1)}, bf16[384,768]{1,0:T(8,128)(2,1)}, u32[]{:S(2)}) copy-start(bf16[384,768]{1,0:T(8,128)(2,1)} %w0.3) | copy-start | bytes 1769476
  0.7 12.5 %collective-permute-start.5 = (bf16[384,384]{1,0:T(8,128)(2,1)}, bf16[384,384]{1,0:T(8,128)(2,1)S(1)}, u32[]{:S(2)}, u32[]{:S(2)}) collective-permute-start(bf16[384,384]{1,0:T(8,128)(2,1)} %bitcast.31), channel_id=1, source_target_pairs={{0,7},{1,0},{2,1},{3,2},{4,3},{5,4},{6,5},{7,6},{8,15},{9,8},{10,9... | collective-permute-start | bytes 884744 | tf_op jit(solution)/shard_map/ppermute | solution.py:288
  6.6 10.2 %collective-permute-start.2 = (bf16[384,384]{1,0:T(8,128)(2,1)}, bf16[384,384]{1,0:T(8,128)(2,1)S(1)}, u32[]{:S(2)}, u32[]{:S(2)}) collective-permute-start(bf16[384,384]{1,0:T(8,128)(2,1)} %bitcast.32), channel_id=1, source_target_pairs={{0,1},{1,2},{2,3},{3,4},{4,5},{5,6},{6,7},{7,0},{8,9},{9,10},{10,1... | collective-permute-start | bytes 884744 | tf_op jit(solution)/shard_map/ppermute | solution.py:287
  7.7 34.4 %copy-start.4 = (s32[1,2]{1,0:T(1,128)S(1)}, s32[1,2]{1,0:T(1,128)}, u32[]{:S(2)}) copy-start(s32[1,2]{1,0:T(1,128)} %param.19) | copy-start | bytes 28
  7.7 34.4 %copy-start.5 = (s32[8,1]{0,1:T(1,128)S(1)}, s32[8,1]{0,1:T(1,128)}, u32[]{:S(2)}) copy-start(s32[8,1]{0,1:T(1,128)} %param.20) | copy-start | bytes 100
  7.7 14.5 %collective-permute-start.12 = (bf16[192,768]{1,0:T(8,128)(2,1)S(1)}, bf16[192,768]{1,0:T(8,128)(2,1)S(1)}, u32[]{:S(2)}, u32[]{:S(2)}) collective-permute-start(bf16[192,768]{1,0:T(8,128)(2,1)S(1)} %get-tuple-element.44), channel_id=1, source_target_pairs={{0,160},{8,168},{16,176},{24,184},{128,0},{136,8},{144,16},{152,24... | collective-permute-start | bytes 884744 | tf_op jit(solution)/shard_map/ppermute | solution.py:302
  8.5 19.0 %collective-permute-start.11 = (bf16[192,768]{1,0:T(8,128)(2,1)S(1)}, bf16[192,768]{1,0:T(8,128)(2,1)S(1)}, u32[]{:S(2)}, u32[]{:S(2)}) collective-permute-start(bf16[192,768]{1,0:T(8,128)(2,1)S(1)} %get-tuple-element.45), channel_id=1, source_target_pairs={{0,128},{8,136},{16,144},{24,152},{128,32},{136,40},{144,48},{152,... | collective-permute-start | bytes 884744 | tf_op jit(solution)/shard_map/ppermute | solution.py:301
  13.2 11.0 %collective-permute-start.6 = (bf16[384,384]{1,0:T(8,128)(2,1)S(1)}, bf16[384,384]{1,0:T(8,128)(2,1)S(1)}, u32[]{:S(2)}, u32[]{:S(2)}) collective-permute-start(bf16[384,384]{1,0:T(8,128)(2,1)S(1)} %collective-permute-done.5.s2), channel_id=1, source_target_pairs={{0,7},{1,0},{2,1},{3,2},{4,3},{5,4},{6,5},{7,6},{8,15},{9,8},{10,9... | collective-permute-start | bytes 884744 | tf_op jit(solution)/shard_map/ppermute | solution.py:288
  16.8 10.7 %collective-permute-start.3 = (bf16[384,384]{1,0:T(8,128)(2,1)S(1)}, bf16[384,384]{1,0:T(8,128)(2,1)S(1)}, u32[]{:S(2)}, u32[]{:S(2)}) collective-permute-start(bf16[384,384]{1,0:T(8,128)(2,1)S(1)} %collective-permute-done.2.s1), channel_id=1, source_target_pairs={{0,1},{1,2},{2,3},{3,4},{4,5},{5,6},{6,7},{7,0},{8,9},{9,10},{10,1... | collective-permute-start | bytes 884744 | tf_op jit(solution)/shard_map/ppermute | solution.py:287
  16.9 18.6 %collective-permute-start.1 = (bf16[2,384,384]{2,1,0:T(8,128)(2,1)S(1)}, bf16[2,384,384]{2,1,0:T(8,128)(2,1)S(1)}, u32[]{:S(2)}, u32[]{:S(2)}) collective-permute-start(bf16[2,384,384]{2,1,0:T(8,128)(2,1)S(1)} %constant_dynamic-update-slice_fusion), channel_id=1, source_target_pairs={{8,0},{16,8},{24,16},{32,24},{40,32},{48,40},{56,48},{9,1},{17,9},... | collective-permute-start | bytes 1769480 | tf_op jit(solution)/shard_map/ppermute | solution.py:295
  22.2 19.2 %collective-permute-start = (bf16[2,384,384]{2,1,0:T(8,128)(2,1)S(1)}, bf16[2,384,384]{2,1,0:T(8,128)(2,1)S(1)}, u32[]{:S(2)}, u32[]{:S(2)}) collective-permute-start(bf16[2,384,384]{2,1,0:T(8,128)(2,1)S(1)} %constant_dynamic-update-slice_fusion), channel_id=1, source_target_pairs={{0,8},{8,16},{16,24},{24,32},{32,40},{40,48},{48,56},{1,9},{9,17},... | collective-permute-start | bytes 1769480 | tf_op jit(solution)/shard_map/ppermute | solution.py:294
  24.2 7.9 %collective-permute-start.7 = (bf16[384,384]{1,0:T(8,128)(2,1)S(1)}, bf16[384,384]{1,0:T(8,128)(2,1)S(1)}, u32[]{:S(2)}, u32[]{:S(2)}) collective-permute-start(bf16[384,384]{1,0:T(8,128)(2,1)S(1)} %collective-permute-done.6.s4), channel_id=1, source_target_pairs={{0,7},{1,0},{2,1},{3,2},{4,3},{5,4},{6,5},{7,6},{8,15},{9,8},{10,9... | collective-permute-start | bytes 884744 | tf_op jit(solution)/shard_map/ppermute | solution.py:288
  27.5 8.0 %collective-permute-start.4 = (bf16[384,384]{1,0:T(8,128)(2,1)S(1)}, bf16[384,384]{1,0:T(8,128)(2,1)S(1)}, u32[]{:S(2)}, u32[]{:S(2)}) collective-permute-start(bf16[384,384]{1,0:T(8,128)(2,1)S(1)} %collective-permute-done.3.s3), channel_id=1, source_target_pairs={{0,1},{1,2},{2,3},{3,4},{4,5},{5,6},{6,7},{7,0},{8,9},{9,10},{10,1... | collective-permute-start | bytes 884744 | tf_op jit(solution)/shard_map/ppermute | solution.py:287
  27.5 20.5 %collective-permute-start.10 = (bf16[384,768]{1,0:T(8,128)(2,1)S(1)}, bf16[384,768]{1,0:T(8,128)(2,1)S(1)}, u32[]{:S(2)}, u32[]{:S(2)}) collective-permute-start(bf16[384,768]{1,0:T(8,128)(2,1)S(1)} %copy-done.6), channel_id=1, source_target_pairs={{0,64},{64,0},{1,65},{65,1},{2,66},{66,2},{3,67},{67,3},{4,68},{68... | collective-permute-start | bytes 1769480 | tf_op jit(solution)/shard_map/ppermute | solution.py:298
  32.1 15.9 %collective-permute-start.14 = (bf16[192,768]{1,0:T(8,128)(2,1)S(1)}, bf16[192,768]{1,0:T(8,128)(2,1)S(1)}, u32[]{:S(2)}, u32[]{:S(2)}) collective-permute-start(bf16[192,768]{1,0:T(8,128)(2,1)S(1)} %collective-permute-done.12.w2b), channel_id=1, source_target_pairs={{0,64},{64,0},{1,65},{65,1},{2,66},{66,2},{3,67},{67,3},{4,68},{68... | collective-permute-start | bytes 884744 | tf_op jit(solution)/shard_map/ppermute | solution.py:304
  35.5 12.5 %collective-permute-start.13 = (bf16[192,768]{1,0:T(8,128)(2,1)S(1)}, bf16[192,768]{1,0:T(8,128)(2,1)S(1)}, u32[]{:S(2)}, u32[]{:S(2)}) collective-permute-start(bf16[192,768]{1,0:T(8,128)(2,1)S(1)} %collective-permute-done.11.w2a), channel_id=1, source_target_pairs={{0,64},{64,0},{1,65},{65,1},{2,66},{66,2},{3,67},{67,3},{4,68},{68... | collective-permute-start | bytes 884744 | tf_op jit(solution)/shard_map/ppermute | solution.py:303
  35.5 12.4 %copy-start.1 = (bf16[2,384,384]{2,1,0:T(8,128)(2,1)}, bf16[2,384,384]{2,1,0:T(8,128)(2,1)S(1)}, u32[]{:S(2)}) copy-start(bf16[2,384,384]{2,1,0:T(8,128)(2,1)S(1)} %collective-permute-done.1.nxt) | copy-start | bytes 1769476
  35.5 15.8 %collective-permute-start.9 = (bf16[192,384]{1,0:T(8,128)(2,1)S(1)}, bf16[192,384]{1,0:T(8,128)(2,1)S(1)}, u32[]{:S(2)}, u32[]{:S(2)}) collective-permute-start(bf16[192,384]{1,0:T(8,128)(2,1)S(1)} %slice.17), channel_id=1, source_target_pairs={{0,7},{1,0},{2,1},{3,2},{4,3},{5,4},{6,5},{7,6},{8,15},{9,8},{10,9... | collective-permute-start | bytes 442376 | tf_op jit(solution)/shard_map/ppermute | solution.py:291
  41.4 6.6 %copy-start.2 = (bf16[2,384,384]{2,1,0:T(8,128)(2,1)}, bf16[2,384,384]{2,1,0:T(8,128)(2,1)S(1)}, u32[]{:S(2)}) copy-start(bf16[2,384,384]{2,1,0:T(8,128)(2,1)S(1)} %collective-permute-done.prev) | copy-start | bytes 1769476
  41.4 9.9 %collective-permute-start.8 = (bf16[192,384]{1,0:T(8,128)(2,1)S(1)}, bf16[192,384]{1,0:T(8,128)(2,1)S(1)}, u32[]{:S(2)}, u32[]{:S(2)}) collective-permute-start(bf16[192,384]{1,0:T(8,128)(2,1)S(1)} %slice.16), channel_id=1, source_target_pairs={{0,1},{1,2},{2,3},{3,4},{4,5},{5,6},{6,7},{7,0},{8,9},{9,10},{10,1... | collective-permute-start | bytes 442376 | tf_op jit(solution)/shard_map/ppermute | solution.py:290
  48.0 6.8 %copy-start = (bf16[384,384]{1,0:T(8,128)(2,1)}, bf16[384,384]{1,0:T(8,128)(2,1)S(1)}, u32[]{:S(2)}) copy-start(bf16[384,384]{1,0:T(8,128)(2,1)S(1)} %get-tuple-element.26.att) | copy-start | bytes 884740
  54.6 3.4 %copy-start.3 = (bf16[384,384]{1,0:T(8,128)(2,1)}, bf16[384,384]{1,0:T(8,128)(2,1)S(1)}, u32[]{:S(2)}) copy-start(bf16[384,384]{1,0:T(8,128)(2,1)S(1)} %get-tuple-element.29.gat) | copy-start | bytes 884740
  54.6 3.1 %collective-permute-start.17 = (bf16[8,2,2,48,384]{4,3,2,1,0:T(8,128)(2,1)S(1)}, bf16[8,2,2,48,384]{4,3,2,1,0:T(8,128)(2,1)S(1)}, u32[]{:S(2)}, u32[]{:S(2)}) collective-permute-start(bf16[8,2,2,48,384]{4,3,2,1,0:T(8,128)(2,1)S(1)} %get-tuple-element.39), channel_id=1, source_target_pairs={{0,64},{64,0},{1,65},{65,1},{2,66},{66,2},{3,67},{67,3},{4,68},{68... | collective-permute-start | bytes 3538952 | tf_op jit(solution)/shard_map/ppermute | solution.py:332
  85.3 37.9 %all-to-all-start.1 = ((bf16[16,80,384]{2,1,0:T(8,128)(2,1)}), bf16[16,80,384]{2,1,0:T(8,128)(2,1)S(1)}, u32[]{:S(2)}, u32[]{:S(2)}) async-start(bf16[16,80,384]{2,1,0:T(8,128)(2,1)} %shard_map.161), calls=%async_computation.1 | async-start | bytes 1966080 | tf_op jit(solution)/shard_map/all_to_all | solution.py:363
  97.6 17.5 %collective-permute-start.15 = (bf16[2,384,384]{2,1,0:T(8,128)(2,1)S(1)}, bf16[2,384,384]{2,1,0:T(8,128)(2,1)S(1)}, u32[]{:S(2)}, u32[]{:S(2)}) collective-permute-start(bf16[2,384,384]{2,1,0:T(8,128)(2,1)S(1)} %get-tuple-element.34), channel_id=1, source_target_pairs={{8,0},{16,8},{24,16},{32,24},{40,32},{48,40},{56,48},{9,1},{17,9},... | collective-permute-start | bytes 1769480 | tf_op jit(solution)/shard_map/ppermute | solution.py:356
  103.1 19.2 %collective-permute-start.16 = (bf16[2,384,384]{2,1,0:T(8,128)(2,1)S(1)}, bf16[2,384,384]{2,1,0:T(8,128)(2,1)S(1)}, u32[]{:S(2)}, u32[]{:S(2)}) collective-permute-start(bf16[2,384,384]{2,1,0:T(8,128)(2,1)S(1)} %get-tuple-element.35), channel_id=1, source_target_pairs={{0,8},{8,16},{16,24},{24,32},{32,40},{40,48},{48,56},{1,9},{9,17},... | collective-permute-start | bytes 1769480 | tf_op jit(solution)/shard_map/ppermute | solution.py:357
